TPU v7x, 128 devices: a whole 4x4x4 slice. The times are simulated.
128 devices in a mesh: gy: 8 (over z, y_hi), gx: 16 (over y_lo, x, core).
Axes of the slice: x: 4, y: 4 (y_hi: 2, y_lo: 2; y = y_hi * 2 + y_lo), z: 4, core: 2. Of those that a mesh axis runs over, the one named last changes fastest.
Arguments:
- coefficients: float32 [9, 256, 512], P(None, 'gy', 'gx'), may hold values from -2.1 to 2.1
- vectors: float32 [256, 512, 2048], P('gy', 'gx'), may hold values from -6 to 6
Outputs:
- normal: float32 [25, 256, 512], P(None, 'gy', 'gx')
- image: float32 [256, 512, 2048], P('gy', 'gx')
All inputs are finite; a program needn't handle non-finite values.
Results may differ from a plain program's by a relative error of at most 0.00002.
Values sent between devices are 32-bit elements; how exact they have to be, the bound alone decides.
A program may use at most 192 MiB of HBM per device.

v0:
```python
import jax
import jax.numpy as jnp
from jax import lax
from jax.sharding import PartitionSpec as P


def from_behind(block, axis, distance):
    devices = range(lax.axis_size(axis))
    route = [(i - distance, i) for i in devices if i - distance in devices]
    return lax.ppermute(block, axis, route)


def extended(cells, sides, width):
    for axis, dim in sides:
        count = lax.axis_size(axis)
        ends = count - 1
        head = lax.slice_in_dim(cells, 0, width, axis=dim)
        tail = lax.slice_in_dim(cells, cells.shape[dim] - width, cells.shape[dim], axis=dim)
        cells = jnp.concatenate(
            [
                lax.ppermute(tail, axis, [(i, (i + 1) % count) for i in range(ends)]),
                cells,
                lax.ppermute(head, axis, [((i + 1) % count, i) for i in range(ends)]),
            ],
            axis=dim,
        )
    return cells


def masked_weights(coefficients):
    rows_dev = coefficients.shape[1]
    cols_dev = coefficients.shape[2]
    total_rows = rows_dev * lax.axis_size("gy")
    total_cols = cols_dev * lax.axis_size("gx")
    row_pos = lax.axis_index("gy") * rows_dev + jnp.arange(rows_dev, dtype=jnp.int32)[:, None]
    col_pos = lax.axis_index("gx") * cols_dev + jnp.arange(cols_dev, dtype=jnp.int32)[None, :]
    pieces = []
    for k in range(9):
        a = k // 3 - 1
        b = k % 3 - 1
        inside = (
            (row_pos + a >= 0)
            & (row_pos + a < total_rows)
            & (col_pos + b >= 0)
            & (col_pos + b < total_cols)
        )
        pieces.append(jnp.where(inside, coefficients[k], jnp.zeros_like(coefficients[k])))
    return jnp.stack(pieces)


def per_device(coefficients, vectors):
    rows_dev = coefficients.shape[1]
    cols_dev = coefficients.shape[2]
    masked = masked_weights(coefficients)
    terms = [jnp.zeros((rows_dev + 2, cols_dev + 2), jnp.float32) for slot in range(25)]
    for k in range(9):
        a = k // 3 - 1
        b = k % 3 - 1
        for m in range(9):
            e = m // 3 - k // 3
            f = m % 3 - k % 3
            slot_index = (e + 2) * 5 + (f + 2)
            product = masked[k] * masked[m]
            terms[slot_index] = terms[slot_index] + jnp.pad(
                product, ((1 + a, 1 - a), (1 + b, 1 - b))
            )
    partial_value = jnp.stack(terms)
    from_above = from_behind(partial_value[:, -1, :], "gy", 1)
    from_below = from_behind(partial_value[:, 0, :], "gy", -1)
    inner = partial_value[:, 1:-1, :]
    inner = inner.at[:, 0, :].add(from_above)
    inner = inner.at[:, -1, :].add(from_below)
    from_left = from_behind(inner[:, :, -1], "gx", 1)
    from_right = from_behind(inner[:, :, 0], "gx", -1)
    normal = inner[:, :, 1:-1]
    normal = normal.at[:, :, 0].add(from_left)
    normal = normal.at[:, :, -1].add(from_right)
    wide = extended(vectors, (("gy", 0), ("gx", 1)), 2)
    image = jnp.zeros_like(vectors)
    for e in range(-2, 3):
        for f in range(-2, 3):
            slot_index = (e + 2) * 5 + (f + 2)
            image = (
                image
                + normal[slot_index][:, :, None]
                * wide[2 + e : 2 + e + rows_dev, 2 + f : 2 + f + cols_dev, :]
            )
    return (normal, image)


def solution(mesh):
    in_specs = (P(None, "gy", "gx"), P("gy", "gx", None))
    out_specs = (P(None, "gy", "gx"), P("gy", "gx", None))
    return jax.shard_map(
        per_device, mesh=mesh, in_specs=in_specs, out_specs=out_specs, check_vma=False
    )
```

profile of v0, /device:TPU:39, one launch (start us, length us, event | category | flops | bytes accessed | tf_op | source)
XLA Modules:
  0.0 208.1 jit_solution(15916457318584421104)
XLA Ops:
  0.7 0.9 fusion.72
  1.6 0.9 fusion.77
  2.5 0.9 fusion.61
  4.3 0.9 fusion.71
  5.2 0.9 fusion.64
  6.1 0.9 fusion.54
  8.8 4.8 %collective-permute-start = (f32[25,34]{1,0:T(8,128)S(1)}, f32[25,34]{1,0:T(8,128)S(1)}, u32[]{:S(2)}, u32[]{:S(2)}) collective-permute-start(f32[25,34]{1,0:T(8,128)S(1)} %bitcast.292), channel_id=1, source_target_pairs={{0,16},{16,32},{32,48},{48,64},{64,80},{80,96},{96,112},{1,17},{17... | collective-permute-start | bytes 10208 | tf_op jit(solution)/shard_map/ppermute | solution.py:10
  13.6 2.9 %collective-permute-start.1 = (f32[25,34]{1,0:T(8,128)S(1)}, f32[25,34]{1,0:T(8,128)S(1)}, u32[]{:S(2)}, u32[]{:S(2)}) collective-permute-start(f32[25,34]{1,0:T(8,128)S(1)} %bitcast.291), channel_id=1, source_target_pairs={{16,0},{32,16},{48,32},{64,48},{80,64},{96,80},{112,96},{17,1},{33... | collective-permute-start | bytes 10208 | tf_op jit(solution)/shard_map/ppermute | solution.py:10
  16.5 2.3 %fusion.80 = (f32[2,32,2048]{2,1,0:T(8,128)}, f32[2,32,2048]{2,1,0:T(8,128)}) fusion(f32[32,32,2048]{2,1,0:T(8,128)} %param.11), kind=kLoop, calls=%fused_computation.184 | loop fusion | bytes 2097152 | tf_op jit(solution)/shard_map/slice | solution.py:18
  18.8 3.9 %collective-permute-start.4 = (f32[2,32,2048]{2,1,0:T(8,128)}, f32[2,32,2048]{2,1,0:T(8,128)S(1)}, u32[]{:S(2)}, u32[]{:S(2)}) collective-permute-start(f32[2,32,2048]{2,1,0:T(8,128)} %get-tuple-element.62), channel_id=1, source_target_pairs={{0,16},{16,32},{32,48},{48,64},{64,80},{80,96},{96,112},{1,17},{17... | collective-permute-start | bytes 1572872 | tf_op jit(solution)/shard_map/ppermute | solution.py:21
  22.7 3.8 %collective-permute-start.5 = (f32[2,32,2048]{2,1,0:T(8,128)}, f32[2,32,2048]{2,1,0:T(8,128)S(1)}, u32[]{:S(2)}, u32[]{:S(2)}) collective-permute-start(f32[2,32,2048]{2,1,0:T(8,128)} %get-tuple-element.63), channel_id=1, source_target_pairs={{16,0},{32,16},{48,32},{64,48},{80,64},{96,80},{112,96},{17,1},{33... | collective-permute-start | bytes 1572872 | tf_op jit(solution)/shard_map/ppermute | solution.py:23
  27.2 3.7 %collective-permute-start.3 = (f32[25,32]{1,0:T(8,128)S(1)}, f32[25,32]{1,0:T(8,128)S(1)}, u32[]{:S(2)}, u32[]{:S(2)}) collective-permute-start(f32[25,32]{1,0:T(8,128)S(1)} %get-tuple-element.54), channel_id=1, source_target_pairs={{1,0},{2,1},{3,2},{4,3},{5,4},{6,5},{7,6},{8,7},{9,8},{10,9},{11,1... | collective-permute-start | bytes 9608 | tf_op jit(solution)/shard_map/ppermute | solution.py:10
  30.9 4.0 %collective-permute-start.2 = (f32[25,32]{1,0:T(8,128)S(1)}, f32[25,32]{1,0:T(8,128)S(1)}, u32[]{:S(2)}, u32[]{:S(2)}) collective-permute-start(f32[25,32]{1,0:T(8,128)S(1)} %get-tuple-element.55), channel_id=1, source_target_pairs={{0,1},{1,2},{2,3},{3,4},{4,5},{5,6},{6,7},{7,8},{8,9},{9,10},{10,1... | collective-permute-start | bytes 9608 | tf_op jit(solution)/shard_map/ppermute | solution.py:10
  34.9 14.2 %constant_dynamic-update-slice_fusion.26 = (f32[34,32,2048]{2,0,1:T(8,128)}, f32[32,32,2048]{2,0,1:T(8,128)}) fusion(f32[32,32,2048]{2,1,0:T(8,128)} %param.11), kind=kLoop, calls=%fused_computation.87 | loop fusion | bytes 25165824
  50.0 2.9 %scatter-add.16 = f32[25,32,32]{2,1,0:T(8,128)S(1)} dynamic-update-slice(f32[25,32,32]{2,1,0:T(8,128)S(1)} %slice.395, f32[25,32,1]{2,1,0:T(8,128)S(1)} %slice_add_fusion.1, s32[]{:T(128)} %constant.126.clone.1, s32[]{:T(128)} %constant.126.clone.1, s32[]{:T(128)} %constant.126.clone.1) | dynamic-update-slice | bytes 6404 | tf_op jit(solution)/shard_map/scatter-add | solution.py:76
  53.3 1.4 constant_dynamic-update-slice_fusion.25
  54.7 2.2 %pad_maximum_fusion.4 = (f32[36,2,2048]{2,0,1:T(8,128)}, f32[36,2,2048]{2,0,1:T(8,128)S(1)}) fusion(f32[2,32,2048]{2,0,1:T(2,128)S(1)} %get-tuple-element.65, f32[32,32,2048]{2,0,1:T(8,128)} %get-tuple-element.61, f32[2,32,2048]{2,0,1:T(2,128)S(1)} %copy.90), kind=kLoop, calls=%fused_computation.56 | loop fusion | flops 589824 | bytes 10616832 | tf_op jit(solution)/shard_map/slice | solution.py:18
  56.9 1.9 collective-permute-start.6
  58.8 2.6 %collective-permute-start.7 = (f32[36,2,2048]{2,0,1:T(8,128)S(1)}, f32[36,2,2048]{2,0,1:T(8,128)}, u32[]{:S(2)}, u32[]{:S(2)}) collective-permute-start(f32[36,2,2048]{2,0,1:T(8,128)S(1)} %get-tuple-element.59), channel_id=1, source_target_pairs={{1,0},{2,1},{3,2},{4,3},{5,4},{6,5},{7,6},{8,7},{9,8},{10,9},{11,1... | collective-permute-start | bytes 1769480 | tf_op jit(solution)/shard_map/ppermute | solution.py:23
  61.6 4.6 %scatter-add.19 = f32[25,32,32]{2,1,0:T(8,128)S(1)} dynamic-update-slice(f32[25,32,32]{2,1,0:T(8,128)S(1)} %scatter-add.16, f32[25,32,1]{2,1,0:T(8,128)S(1)} %slice_add_fusion, s32[]{:T(128)} %constant.126.clone.1, s32[]{:T(128)} %constant.126.clone.1, s32[]{:T(128)} %constant.132.clone.1) | dynamic-update-slice | bytes 6404 | tf_op jit(solution)/shard_map/scatter-add | solution.py:77
  68.1 4.9 %collective-permute-done.7 = f32[36,2,2048]{2,0,1:T(8,128)} collective-permute-done((f32[36,2,2048]{2,0,1:T(8,128)S(1)}, f32[36,2,2048]{2,0,1:T(8,128)}, u32[]{:S(2)}, u32[]{:S(2)}) %collective-permute-start.7) | collective-permute-done | bytes 589856 | tf_op jit(solution)/shard_map/ppermute | solution.py:23
  72.9 14.3 %maximum_maximum_fusion = (f32[36,34,2048]{2,0,1:T(8,128)}, f32[36,34,2048]{2,0,1:T(8,128)}) fusion(f32[2,32,2048]{2,0,1:T(2,128)S(1)} %get-tuple-element.65, f32[32,32,2048]{2,0,1:T(8,128)} %get-tuple-element.61, f32[2,32,2048]{2,0,1:T(2,128)S(1)} %copy.90, f32[36,2,2048]{2,0,1:T(8,128)} %collective-permute-done.6, f32[36,2,2048]{2,0,1:T(8,128)} %collective-permute-done.7), kind=kLoop, calls=%fused_computation | loop fusion | flops 15040512 | bytes 30670848 | tf_op jit(solution)/shard_map/concatenate | solution.py:19
  87.3 109.2 %fusion.24 = f32[32,32,2048]{2,0,1:T(8,128)} fusion(f32[36,34,2048]{2,0,1:T(8,128)} %get-tuple-element.57, f32[34,32,2048]{2,0,1:T(8,128)} %get-tuple-element.64, f32[36,34,2048]{2,0,1:T(8,128)} %get-tuple-element.56, f32[32,32,2048]{2,0,1:T(8,128)} %get-tuple-element.61, f32[2,32,2048]{2,0,1:T(2,128)S(1)} %copy.90, f32[32,32]{0,1:T(8,128)S(1)} %copy.121, ...), kind=kLoop, calls=%fused_computation.29 | loop fusion | flops 106954752 | bytes 201953280 | tf_op jit(solution)/shard_map/add | solution.py:84
  196.5 11.6 %copy.122 = f32[32,32,2048]{2,1,0:T(8,128)} copy(f32[32,32,2048]{2,0,1:T(8,128)} %fusion.24) | data formatting | bytes 16777216
  (83 shorter events, 6.5 us)
Async XLA Ops:
  8.8 17.8 %collective-permute-start = (f32[25,34]{1,0:T(8,128)S(1)}, f32[25,34]{1,0:T(8,128)S(1)}, u32[]{:S(2)}, u32[]{:S(2)}) collective-permute-start(f32[25,34]{1,0:T(8,128)S(1)} %bitcast.292), channel_id=1, source_target_pairs={{0,16},{16,32},{32,48},{48,64},{64,80},{80,96},{96,112},{1,17},{17... | collective-permute-start | bytes 10208 | tf_op jit(solution)/shard_map/ppermute | solution.py:10
  13.6 13.1 %collective-permute-start.1 = (f32[25,34]{1,0:T(8,128)S(1)}, f32[25,34]{1,0:T(8,128)S(1)}, u32[]{:S(2)}, u32[]{:S(2)}) collective-permute-start(f32[25,34]{1,0:T(8,128)S(1)} %bitcast.291), channel_id=1, source_target_pairs={{16,0},{32,16},{48,32},{64,48},{80,64},{96,80},{112,96},{17,1},{33... | collective-permute-start | bytes 10208 | tf_op jit(solution)/shard_map/ppermute | solution.py:10
  18.8 34.0 %collective-permute-start.4 = (f32[2,32,2048]{2,1,0:T(8,128)}, f32[2,32,2048]{2,1,0:T(8,128)S(1)}, u32[]{:S(2)}, u32[]{:S(2)}) collective-permute-start(f32[2,32,2048]{2,1,0:T(8,128)} %get-tuple-element.62), channel_id=1, source_target_pairs={{0,16},{16,32},{32,48},{48,64},{64,80},{80,96},{96,112},{1,17},{17... | collective-permute-start | bytes 1572872 | tf_op jit(solution)/shard_map/ppermute | solution.py:21
  22.7 30.5 %collective-permute-start.5 = (f32[2,32,2048]{2,1,0:T(8,128)}, f32[2,32,2048]{2,1,0:T(8,128)S(1)}, u32[]{:S(2)}, u32[]{:S(2)}) collective-permute-start(f32[2,32,2048]{2,1,0:T(8,128)} %get-tuple-element.63), channel_id=1, source_target_pairs={{16,0},{32,16},{48,32},{64,48},{80,64},{96,80},{112,96},{17,1},{33... | collective-permute-start | bytes 1572872 | tf_op jit(solution)/shard_map/ppermute | solution.py:23
  27.2 22.3 %collective-permute-start.3 = (f32[25,32]{1,0:T(8,128)S(1)}, f32[25,32]{1,0:T(8,128)S(1)}, u32[]{:S(2)}, u32[]{:S(2)}) collective-permute-start(f32[25,32]{1,0:T(8,128)S(1)} %get-tuple-element.54), channel_id=1, source_target_pairs={{1,0},{2,1},{3,2},{4,3},{5,4},{6,5},{7,6},{8,7},{9,8},{10,9},{11,1... | collective-permute-start | bytes 9608 | tf_op jit(solution)/shard_map/ppermute | solution.py:10
  30.9 18.4 %collective-permute-start.2 = (f32[25,32]{1,0:T(8,128)S(1)}, f32[25,32]{1,0:T(8,128)S(1)}, u32[]{:S(2)}, u32[]{:S(2)}) collective-permute-start(f32[25,32]{1,0:T(8,128)S(1)} %get-tuple-element.55), channel_id=1, source_target_pairs={{0,1},{1,2},{2,3},{3,4},{4,5},{5,6},{6,7},{7,8},{8,9},{9,10},{10,1... | collective-permute-start | bytes 9608 | tf_op jit(solution)/shard_map/ppermute | solution.py:10
  56.9 11.2 %collective-permute-start.6 = (f32[36,2,2048]{2,0,1:T(8,128)}, f32[36,2,2048]{2,0,1:T(8,128)}, u32[]{:S(2)}, u32[]{:S(2)}) collective-permute-start(f32[36,2,2048]{2,0,1:T(8,128)} %get-tuple-element.58), channel_id=1, source_target_pairs={{0,1},{1,2},{2,3},{3,4},{4,5},{5,6},{6,7},{7,8},{8,9},{9,10},{10,1... | collective-permute-start | bytes 1769480 | tf_op jit(solution)/shard_map/ppermute | solution.py:21
  58.8 14.1 %collective-permute-start.7 = (f32[36,2,2048]{2,0,1:T(8,128)S(1)}, f32[36,2,2048]{2,0,1:T(8,128)}, u32[]{:S(2)}, u32[]{:S(2)}) collective-permute-start(f32[36,2,2048]{2,0,1:T(8,128)S(1)} %get-tuple-element.59), channel_id=1, source_target_pairs={{1,0},{2,1},{3,2},{4,3},{5,4},{6,5},{7,6},{8,7},{9,8},{10,9},{11,1... | collective-permute-start | bytes 1769480 | tf_op jit(solution)/shard_map/ppermute | solution.py:23
  66.2 21.1 %copy-start = (f32[25,32,32]{2,1,0:T(8,128)}, f32[25,32,32]{2,1,0:T(8,128)S(1)}, u32[]{:S(2)}) copy-start(f32[25,32,32]{2,1,0:T(8,128)S(1)} %scatter-add.19) | copy-start | bytes 307204
where the time goes:
time: 209 us; the launch traced here: 208 us
  other arithmetic  134 us (64%)
  local copies, waits for them, and re-layouts  40.7 us (19%)
  starting transfers between devices  27.5 us (13%)
  waiting for transfers between devices  4.89 us (2%)
    add x1, other arithmetic, per_device(): image + normal[slot_index][:, :, None] * wide[2 + e:2 + e + rows_dev, 2 +...  109 us
    unnamed x9, local copies, waits for them, and re-layouts  26 us
    ppermute x4, starting transfers between devices, from_behind(): return lax.ppermute(block, axis, route)  15.4 us
    concatenate x1, other arithmetic, extended(): jnp.concatenate([lax.ppermute(tail, axis, [(i, (i + 1) % count) for i in...  14.3 us
    ppermute x2, starting transfers between devices, extended(): lax.ppermute(head, axis, [((i + 1) % count, i) for i in range(ends)])  6.35 us
    mul x7, other arithmetic, per_device(): product = masked[k] * masked[m]  6.18 us
    ppermute x2, starting transfers between devices, extended(): lax.ppermute(tail, axis, [(i, (i + 1) % count) for i in range(ends)])  5.82 us
    ppermute x2, waiting for transfers between devices, extended(): lax.ppermute(head, axis, [((i + 1) % count, i) for i in range(ends)])  4.87 us
  transfers between devices with their start and end apart: 8, of which 1 were waited for; matrix products, arithmetic and copies ran while one was open for 13% of the time, Pallas kernels for 0%

commit v1 on v0

v1 whole, which is shorter than its diff:
```python
import functools

import jax
import jax.numpy as jnp
from jax import lax
from jax.experimental import pallas as pl
from jax.experimental.pallas import tpu as pltpu
from jax.sharding import PartitionSpec as P

MESH = pl.DeviceIdType.MESH
F32 = jnp.float32
BF16 = jnp.bfloat16
STEPS = ((-1, 0), (1, 0), (0, -1), (0, 1), (-1, -1), (-1, 1), (1, -1), (1, 1))
UP, DOWN, LEFT, RIGHT = 0, 1, 2, 3
CHUNKS = 8
SLOTS = [((m // 3 - k // 3) + 2) * 5 + (m % 3 - k % 3) + 2 for k in range(9) for m in range(9)]


def kernel(
    rows_total, cols_total,
    coef_hbm, v_hbm, normal_ref, image_ref,
    coef, padded, flipped, shifted, nts,
    v_vm, up_vm, down_vm, col_vm, col_out, corner_out,
    row_msg, col_msg, heard,
    t_hi, t_lo, w_hi, w_lo,
    load_sem, coef_sem, msg_send, msg_recv, row_send, row_recv, col_send, col_recv, cor_send, cor_recv,
):
    gy = lax.axis_index("gy")
    gx = lax.axis_index("gx")
    ny = lax.axis_size("gy")
    nx = lax.axis_size("gx")
    rows, cols, nv = v_hbm.shape
    width = nv // CHUNKS

    def exists(n):
        dy, dx = STEPS[n]
        return (gy + dy >= 0) & (gy + dy < ny) & (gx + dx >= 0) & (gx + dx < nx)

    def at(n):
        dy, dx = STEPS[n]
        return (gy + dy, gx + dx)

    def lanes(i):
        return pl.ds(pl.multiple_of(i * width, width), width)

    def load(i):
        return pltpu.make_async_copy(v_hbm.at[:, :, lanes(i)], v_vm.at[:, :, lanes(i)], load_sem.at[i])

    def row_copy(s, i):
        src = v_hbm.at[0:2, :, lanes(i)] if s == UP else v_hbm.at[rows - 2:rows, :, lanes(i)]
        dst = down_vm if s == UP else up_vm
        return pltpu.make_async_remote_copy(
            src_ref=src, dst_ref=dst.at[:, :, lanes(i)], send_sem=row_send.at[s, i],
            recv_sem=row_recv.at[s, i], device_id=at(s), device_id_type=MESH)

    def col_copy(s, i):
        j = 2 - 2 * s
        return pltpu.make_async_remote_copy(
            src_ref=col_out.at[s, :, :, lanes(i)], dst_ref=col_vm.at[j:j + 2, 0:rows, lanes(i)],
            send_sem=col_send.at[s, i], recv_sem=col_recv.at[s, i], device_id=at(LEFT + s), device_id_type=MESH)

    def cor_copy(s, i):
        j = 2 - 2 * s
        return pltpu.make_async_remote_copy(
            src_ref=corner_out.at[s, :, :, lanes(i)], dst_ref=col_vm.at[j:j + 2, rows:rows + 8, lanes(i)],
            send_sem=cor_send.at[s, i], recv_sem=cor_recv.at[s, i], device_id=at(LEFT + s), device_id_type=MESH)

    def msg_copy(n):
        dy, dx = STEPS[n]
        src = row_msg.at[(dy + 1) // 2] if dy else col_msg.at[(dx + 1) // 2]
        return pltpu.make_async_remote_copy(
            src_ref=src, dst_ref=heard.at[n], send_sem=msg_send.at[n], recv_sem=msg_recv.at[n],
            device_id=at(n), device_id_type=MESH)

    opposite = [STEPS.index((-dy, -dx)) for dy, dx in STEPS]

    def when(pred, f):
        pl.when(pred)(f)

    take_coef = pltpu.make_async_copy(coef_hbm, coef, coef_sem)
    take_coef.start()
    for i in range(CHUNKS):
        load(i).start()

    barrier = pltpu.get_barrier_semaphore()
    known = jnp.int32(0)
    for n in range(8):
        when(exists(n), lambda n=n: pl.semaphore_signal(barrier, inc=1, device_id=at(n), device_id_type=MESH))
        known = known + exists(n).astype(jnp.int32)
    pl.semaphore_wait(barrier, known)

    def send_rows(i):
        for s in (UP, DOWN):
            when(exists(s), lambda s=s: row_copy(s, i).start())

    send_rows(0)
    padded[...] = jnp.zeros_like(padded)
    row_msg[...] = jnp.zeros_like(row_msg)
    col_msg[...] = jnp.zeros_like(col_msg)
    flipped[...] = jnp.zeros_like(flipped)
    take_coef.wait()
    padded[0:9, :, 0:cols] = coef[...]
    lane = lax.broadcasted_iota(jnp.int32, (8, 128), 1)
    for e, r in ((0, 0), (1, rows - 1)):
        for k in range(8):
            row_msg[e, k:k + 1, :] = padded[k, r:r + 1, :]
        last = pltpu.roll(jnp.broadcast_to(padded[8, r:r + 1, :], (8, 128)), 32, 1)
        row_msg[e] = jnp.where((lane >= 32) & (lane < 64), last, row_msg[e])
    for g in range(3):
        turned = padded[4 * g:4 * g + 4].reshape(128, 128).T
        col_msg[0, g:g + 1, :] = turned[0:1]
        col_msg[1, g:g + 1, :] = turned[cols - 1:cols]
        flipped[g, 1:cols + 1, :] = turned[0:cols]
    for n in range(8):
        when(exists(n), lambda n=n: msg_copy(n).start())

    def rest(i, c):
        send_rows(i)
        return c

    lax.fori_loop(1, CHUNKS, rest, 0)

    corner_out[...] = jnp.zeros_like(corner_out)

    def clear(ref):
        ref[...] = jnp.zeros_like(ref)

    when(jnp.logical_not(exists(UP)), lambda: clear(up_vm))
    when(jnp.logical_not(exists(DOWN)), lambda: clear(down_vm))
    when(jnp.logical_not(exists(LEFT)), lambda: clear(col_vm.at[0:2]))
    when(jnp.logical_not(exists(RIGHT)), lambda: clear(col_vm.at[2:4]))

    def pack(i, c):
        load(i).wait()
        for s in (0, 1):
            for j in (0, 1):
                col = j if s == 0 else cols - 2 + j
                for r in range(0, rows, 8):
                    col_out[s, j, r:r + 8, lanes(i)] = v_vm[r:r + 8, col, lanes(i)]
        for s in (0, 1):
            when(exists(LEFT + s), lambda s=s: col_copy(s, i).start())
        return c

    lax.fori_loop(0, CHUNKS, pack, 0)

    for n in range(8):
        when(exists(opposite[n]), lambda n=n: msg_copy(n).wait_recv())

    def from_side(n):
        return heard[opposite[n]]

    for g in range(3):
        flipped[g, 0:1, :] = jnp.where(exists(LEFT), from_side(LEFT)[g:g + 1], 0.0)
        flipped[g, cols + 1:cols + 2, :] = jnp.where(exists(RIGHT), from_side(RIGHT)[g:g + 1], 0.0)

    def rim(side, left, right):
        out = []
        for own, a, b in ((1, 97, 33), (97, 65, 1)):
            x = jnp.where(exists(side), pltpu.roll(from_side(side), own, 1), 0.0)
            x = jnp.where((lane == 0), jnp.where(exists(left), pltpu.roll(from_side(left), a, 1), 0.0), x)
            x = jnp.where((lane == cols + 1), jnp.where(exists(right), pltpu.roll(from_side(right), b, 1), 0.0), x)
            out.append(x)
        return out

    above = rim(UP, 4, 5)
    below = rim(DOWN, 6, 7)
    er = lax.broadcasted_iota(jnp.int32, (40, 128), 0)
    ec = lax.broadcasted_iota(jnp.int32, (40, 128), 1)
    row_at = gy * rows + er - 1
    col_at = gx * cols + ec - 1
    inside = (er < rows + 2) & (ec < cols + 2) & (row_at >= 0) & (row_at < rows_total) & (col_at >= 0) & (col_at < cols_total)
    for g in range(3):
        back = flipped[g].T
        for h in range(4):
            k = 4 * g + h
            if k < 9:
                a, b = k // 3 - 1, k % 3 - 1
                shifted[0, k, 1:rows + 1, :] = back[32 * h:32 * h + rows]
                which, line = (0, k) if k < 8 else (1, 0)
                shifted[0, k, 0:1, :] = above[which][line:line + 1]
                shifted[0, k, rows + 1:rows + 2, :] = below[which][line:line + 1]
                keep = inside & (row_at + a >= 0) & (row_at + a < rows_total) & (col_at + b >= 0) & (col_at + b < cols_total)
                x = jnp.where(keep, shifted[0, k], 0.0)
                shifted[0, k] = x
                shifted[1, k] = pltpu.roll(x, 127, 1)
                shifted[2, k] = pltpu.roll(x, 126, 1)
    terms = []
    for slot in range(25):
        total = None
        for at_pair in range(81):
            if SLOTS[at_pair] == slot:
                k, m = at_pair // 9, at_pair % 9
                a, b = k // 3 - 1, k % 3 - 1
                term = shifted[1 - b, k, 1 - a:1 - a + rows, :] * shifted[1 - b, m, 1 - a:1 - a + rows, :]
                total = term if total is None else total + term
        normal_ref[slot] = total[:, 0:cols]
        terms.append(total)
    for g in range(7):
        group = terms[4 * g:4 * g + 4]
        while len(group) < 4:
            group.append(jnp.zeros_like(group[0]))
        turned = jnp.concatenate(group, axis=0).T[0:cols]
        nts[0, g] = turned
        for b in range(1, 4):
            nts[b, g] = pltpu.roll(turned, 128 - 8 * b, 1)

    lane32 = lax.broadcasted_iota(jnp.int32, (cols, 128), 1)
    cell = lax.broadcasted_iota(jnp.int32, (cols, 128), 0)
    own_at, side_at = {}, {}
    for f in range(-2, 3):
        t = cell + f
        own_at[f] = jnp.where((t >= 0) & (t < cols), t, -1000)
        side_at[f] = jnp.where(t == -2, 0, jnp.where(t == -1, 32, jnp.where(t == cols, 64, jnp.where(t == cols + 1, 96, -1000))))

    def build(b, c):
        for rl in range(8):
            own = [jnp.zeros((cols, 128), F32) for _ in range(3)]
            side = jnp.zeros((cols, 128), F32)
            for e in range(-2, 3):
                spot = rl + e + 2
                tile, q = spot // 4, spot % 4
                row = b * 8 + rl + e
                slot = jnp.where(row < 0, 18 + row, row)
                slot = jnp.where(b == 3, jnp.where(row < rows, row - 16, row - 14), slot)
                for f in range(-2, 3):
                    index = (e + 2) * 5 + f + 2
                    at_lane = (index % 4) * 32 + rl
                    column = jnp.broadcast_to(nts[b, index // 4][:, at_lane:at_lane + 1], (cols, 128))
                    own[tile] = jnp.where(lane32 - 32 * q == own_at[f], column, own[tile])
                    if f:
                        side = jnp.where(lane32 - slot == side_at[f], column, side)
            for tile, x in enumerate(own + [side]):
                hi = x.astype(BF16)
                t_hi[b, rl * 32:rl * 32 + 32, tile * 128:tile * 128 + 128] = hi
                t_lo[b, rl * 32:rl * 32 + 32, tile * 128:tile * 128 + 128] = (x - hi.astype(F32)).astype(BF16)
        return c

    lax.fori_loop(0, 4, build, 0)

    def halves(x):
        hi = x.astype(BF16)
        return hi, (x - hi.astype(F32)).astype(BF16)

    def put(block, start, hi, lo):
        w_hi[block, start:start + hi.shape[0], :] = hi
        w_lo[block, start:start + hi.shape[0], :] = lo

    def compute(i):
        at_i = lanes(i)
        for s in (0, 1):
            when(exists(LEFT + 1 - s), lambda s=s: (col_copy(s, i).wait_recv(), cor_copy(s, i).wait_recv())[0])
        for q in range(4):
            hi, lo = halves(v_vm[8 * q:8 * q + 8, :, at_i].reshape(256, width))
            put(q, 64, hi, lo)
            if q > 0:
                put(q - 1, 320, hi[0:64], lo[0:64])
            if q < 3:
                put(q + 1, 0, hi[192:256], lo[192:256])
        put(0, 0, *halves(up_vm[:, :, at_i].reshape(64, width)))
        put(3, 320, *halves(down_vm[:, :, at_i].reshape(64, width)))
        for j in range(4):
            hi, lo = halves(col_vm[j, 0:32, at_i])
            chi, clo = halves(jnp.concatenate([col_vm[j, 32:40, at_i], jnp.zeros((8, width), F32)], axis=0))
            put(0, 384 + 32 * j, hi[0:16], lo[0:16])
            put(0, 400 + 32 * j, chi, clo)
            put(1, 384 + 32 * j, hi, lo)
            put(2, 384 + 32 * j, hi, lo)
            put(3, 384 + 32 * j, hi[16:32], lo[16:32])
            put(3, 400 + 32 * j, chi, clo)
        for q in range(4):
            y = jnp.dot(t_hi[q], w_hi[q], preferred_element_type=F32)
            y = y + jnp.dot(t_lo[q], w_hi[q], preferred_element_type=F32)
            y = y + jnp.dot(t_hi[q], w_lo[q], preferred_element_type=F32)
            image_ref[8 * q:8 * q + 8, :, at_i] = y.reshape(8, cols, width)

    def main(i, c):
        for s in (UP, DOWN):
            when(exists(1 - s), lambda s=s: row_copy(s, i).wait_recv())
        for s in (0, 1):
            for j in (0, 1):
                col = j if s == 0 else cols - 2 + j
                for h in (0, 1):
                    corner_out[s, j, h:h + 1, lanes(i)] = up_vm[h, col:col + 1, lanes(i)]
                    corner_out[s, j, 2 + h:3 + h, lanes(i)] = down_vm[h, col:col + 1, lanes(i)]
            when(exists(LEFT + s), lambda s=s: cor_copy(s, i).start())
        when(i > 0, lambda: compute(i - 1))
        return c

    lax.fori_loop(0, CHUNKS, main, 0)
    compute(CHUNKS - 1)

    def finish(i, c):
        for s in (0, 1):
            when(exists(s), lambda s=s: row_copy(s, i).wait_send())
            when(exists(LEFT + s), lambda s=s: (col_copy(s, i).wait_send(), cor_copy(s, i).wait_send())[0])
        return c

    lax.fori_loop(0, CHUNKS, finish, 0)
    for n in range(8):
        when(exists(n), lambda n=n: msg_copy(n).wait_send())


def per_device(rows_total, cols_total, coefficients, vectors):
    _, rows, cols = coefficients.shape
    nv = vectors.shape[2]
    width = nv // CHUNKS
    dma = pltpu.SemaphoreType.DMA
    return pl.pallas_call(
        functools.partial(kernel, rows_total, cols_total),
        out_shape=(pltpu.VMEM((25, rows, cols), F32), pltpu.VMEM((rows, cols, nv), F32)),
        in_specs=[pl.BlockSpec(memory_space=pltpu.HBM)] * 2,
        out_specs=(pl.BlockSpec(memory_space=pltpu.VMEM),) * 2,
        scratch_shapes=[
            pltpu.VMEM((9, rows, cols), F32),
            pltpu.VMEM((12, rows, 128), F32),
            pltpu.VMEM((3, 128, 128), F32),
            pltpu.VMEM((3, 9, 40, 128), F32),
            pltpu.VMEM((4, 7, cols, 128), F32),
            pltpu.VMEM((rows, cols, nv), F32),
            pltpu.VMEM((2, cols, nv), F32),
            pltpu.VMEM((2, cols, nv), F32),
            pltpu.VMEM((4, rows + 8, nv), F32),
            pltpu.VMEM((2, 2, rows, nv), F32),
            pltpu.VMEM((2, 2, 8, nv), F32),
            pltpu.VMEM((2, 8, 128), F32),
            pltpu.VMEM((2, 8, 128), F32),
            pltpu.VMEM((8, 8, 128), F32),
            pltpu.VMEM((4, 256, 512), BF16),
            pltpu.VMEM((4, 256, 512), BF16),
            pltpu.VMEM((4, 512, width), BF16),
            pltpu.VMEM((4, 512, width), BF16),
            dma((CHUNKS,)), dma,
            dma((8,)), dma((8,)),
            dma((2, CHUNKS)), dma((2, CHUNKS)),
            dma((2, CHUNKS)), dma((2, CHUNKS)),
            dma((2, CHUNKS)), dma((2, CHUNKS)),
        ],
        compiler_params=pltpu.CompilerParams(collective_id=0, has_side_effects=True, vmem_limit_bytes=44 * 2**20),
    )(coefficients, vectors)


def solution(mesh):
    in_specs = (P(None, "gy", "gx"), P("gy", "gx", None))
    out_specs = (P(None, "gy", "gx"), P("gy", "gx", None))

    def whole(coefficients, vectors):
        body = functools.partial(per_device, coefficients.shape[1], coefficients.shape[2])
        return jax.shard_map(body, mesh=mesh, in_specs=in_specs, out_specs=out_specs, check_vma=False)(coefficients, vectors)

    return whole
```

time: 209 us -> 46.7 us (0.22)
  the two profiles are of different devices: /device:TPU:39 before, /device:TPU:109 now
where the time goes in v1:
time: 46.7 us; the launch traced here: 46.6 us
  Pallas kernels  40.9 us (88%)
  local copies, waits for them, and re-layouts  5.05 us (11%)
  between operations  0.65 us (1%)
    pallas_call x1, Pallas kernels, per_device(): pl.pallas_call(functools.partial(kernel, rows_total, cols_total), out_sha...  40.9 us
    unnamed x4, local copies, waits for them, and re-layouts  5.05 us

profile of v1, /device:TPU:109, one launch (start us, length us, event | category | flops | bytes accessed | tf_op | source)
XLA Modules:
  0.0 46.6 jit_solution(17023064950611401335)
XLA Ops:
  0.6 0.0 copy-start
  0.6 0.9 %copy-done = f32[9,32,32]{2,1,0:T(8,128)S(1)} copy-done((f32[9,32,32]{2,1,0:T(8,128)S(1)}, f32[9,32,32]{2,1,0:T(8,128)}, u32[]{:S(2)}) %copy-start) | copy-done | bytes 36888
  1.5 40.9 %shard_map.41 = (f32[25,32,32]{2,1,0:T(8,128)S(1)}, f32[32,32,2048]{2,1,0:T(8,128)S(1)}) custom-call(f32[9,32,32]{2,1,0:T(8,128)S(1)} %copy-done, f32[32,32,2048]{2,1,0:T(8,128)} %v_hbm.1), custom_call_target="tpu_custom_call" | custom-call | tf_op jit(solution)/shard_map/pallas_call | solution.py:308
  42.4 0.8 %copy.6 = f32[25,32,32]{2,1,0:T(8,128)} copy(f32[25,32,32]{2,1,0:T(8,128)S(1)} %get-tuple-element.2) | data formatting | bytes 204800
  43.2 3.4 %copy.7 = f32[32,32,2048]{2,1,0:T(8,128)} copy(f32[32,32,2048]{2,1,0:T(8,128)S(1)} %get-tuple-element.3) | data formatting | bytes 16777216
Async XLA Ops:
  0.6 0.9 %copy-start = (f32[9,32,32]{2,1,0:T(8,128)S(1)}, f32[9,32,32]{2,1,0:T(8,128)}, u32[]{:S(2)}) copy-start(f32[9,32,32]{2,1,0:T(8,128)} %coef_hbm.1) | copy-start | bytes 110596

commit v2 on v1

--- a/solution.py
+++ b/solution.py
@@ -16,14 +16,19 @@
 SLOTS = [((m // 3 - k // 3) + 2) * 5 + (m % 3 - k % 3) + 2 for k in range(9) for m in range(9)]
 
 
+RELAYS = (12, 11), (3, 4)
+TURN = 7
+
+
 def kernel(
     rows_total, cols_total,
     coef_hbm, v_hbm, normal_ref, image_ref,
     coef, padded, flipped, shifted, nts,
-    v_vm, up_vm, down_vm, col_vm, col_out, corner_out,
+    v_vm, up_vm, down_vm, col_vm, col_out, corner_out, relay_vm,
     row_msg, col_msg, heard,
     t_hi, t_lo, w_hi, w_lo,
     load_sem, coef_sem, msg_send, msg_recv, row_send, row_recv, col_send, col_recv, cor_send, cor_recv,
+    relay_recv, relay_send,
 ):
     gy = lax.axis_index("gy")
     gx = lax.axis_index("gx")
@@ -59,6 +64,46 @@
             src_ref=col_out.at[s, :, :, lanes(i)], dst_ref=col_vm.at[j:j + 2, 0:rows, lanes(i)],
             send_sem=col_send.at[s, i], recv_sem=col_recv.at[s, i], device_id=at(LEFT + s), device_id_type=MESH)
 
+    turns = ((gx == TURN + 1), (gx == TURN))
+
+    def detour(s, i):
+        first, second = RELAYS[1 - s]
+        via = jnp.where(i % 3 == 0, first, second)
+        return pltpu.make_async_remote_copy(
+            src_ref=col_out.at[s, :, :, lanes(i)], dst_ref=relay_vm.at[i // 3],
+            send_sem=col_send.at[s, i], recv_sem=relay_recv.at[i // 3], device_id=(gy, via), device_id_type=MESH)
+
+    def send_cols(s, i):
+        around = turns[s] & (i % 3 < 2)
+        when(exists(LEFT + s) & jnp.logical_not(around), lambda: col_copy(s, i).start())
+        when(around, lambda: detour(s, i).start())
+
+    def forward(s, i):
+        j = 2 - 2 * s
+        return pltpu.make_async_remote_copy(
+            src_ref=relay_vm.at[i // 3], dst_ref=col_vm.at[j:j + 2, 0:rows, lanes(i)],
+            send_sem=relay_send.at[i // 3], recv_sem=col_recv.at[s, i], device_id=(gy, TURN + s), device_id_type=MESH)
+
+    def relays(f):
+        for s in (0, 1):
+            for n, via in enumerate(RELAYS[1 - s]):
+                when(gx == via, functools.partial(f, s, n))
+
+    def pass_on(j):
+        def one(s, n):
+            i = n + 3 * j
+            if i < CHUNKS:
+                detour(s, i).wait_recv()
+                forward(s, i).start()
+        relays(one)
+
+    def passed_on(j):
+        def one(s, n):
+            i = n + 3 * j
+            if i < CHUNKS:
+                forward(s, i).wait_send()
+        relays(one)
+
     def cor_copy(s, i):
         j = 2 - 2 * s
         return pltpu.make_async_remote_copy(
@@ -87,6 +132,12 @@
     for n in range(8):
         when(exists(n), lambda n=n: pl.semaphore_signal(barrier, inc=1, device_id=at(n), device_id_type=MESH))
         known = known + exists(n).astype(jnp.int32)
+    for side in RELAYS:
+        for via in side:
+            for end in (TURN, TURN + 1):
+                for me, other in ((via, end), (end, via)):
+                    when(gx == me, lambda other=other: pl.semaphore_signal(barrier, inc=1, device_id=(gy, other), device_id_type=MESH))
+                    known = known + (gx == me).astype(jnp.int32)
     pl.semaphore_wait(barrier, known)
 
     def send_rows(i):
@@ -138,7 +189,7 @@
                 for r in range(0, rows, 8):
                     col_out[s, j, r:r + 8, lanes(i)] = v_vm[r:r + 8, col, lanes(i)]
         for s in (0, 1):
-            when(exists(LEFT + s), lambda s=s: col_copy(s, i).start())
+            send_cols(s, i)
         return c
 
     lax.fori_loop(0, CHUNKS, pack, 0)
@@ -235,7 +286,11 @@
                 t_lo[b, rl * 32:rl * 32 + 32, tile * 128:tile * 128 + 128] = (x - hi.astype(F32)).astype(BF16)
         return c
 
-    lax.fori_loop(0, 4, build, 0)
+    pass_on(0)
+    lax.fori_loop(0, 2, build, 0)
+    pass_on(1)
+    lax.fori_loop(2, 4, build, 0)
+    pass_on(2)
 
     def halves(x):
         hi = x.astype(BF16)
@@ -298,6 +353,8 @@
     lax.fori_loop(0, CHUNKS, finish, 0)
     for n in range(8):
         when(exists(n), lambda n=n: msg_copy(n).wait_send())
+    for j in range(3):
+        passed_on(j)
 
 
 def per_device(rows_total, cols_total, coefficients, vectors):
@@ -322,6 +379,7 @@
             pltpu.VMEM((4, rows + 8, nv), F32),
             pltpu.VMEM((2, 2, rows, nv), F32),
             pltpu.VMEM((2, 2, 8, nv), F32),
+            pltpu.VMEM((3, 2, rows, width), F32),
             pltpu.VMEM((2, 8, 128), F32),
             pltpu.VMEM((2, 8, 128), F32),
             pltpu.VMEM((8, 8, 128), F32),
@@ -334,6 +392,7 @@
             dma((2, CHUNKS)), dma((2, CHUNKS)),
             dma((2, CHUNKS)), dma((2, CHUNKS)),
             dma((2, CHUNKS)), dma((2, CHUNKS)),
+            dma((3,)), dma((3,)),
         ],
         compiler_params=pltpu.CompilerParams(collective_id=0, has_side_effects=True, vmem_limit_bytes=44 * 2**20),
     )(coefficients, vectors)

time: 46.7 us -> 43 us (0.921)
  the two profiles are of different devices: /device:TPU:109 before, /device:TPU:39 now
where the time goes in v2:
time: 43 us; the launch traced here: 42.3 us
  Pallas kernels  36.6 us (85%)
  local copies, waits for them, and re-layouts  5.05 us (12%)
  between operations  0.65 us (2%)
    pallas_call x1, Pallas kernels, per_device(): pl.pallas_call(functools.partial(kernel, rows_total, cols_total), out_sha...  36.6 us
    unnamed x4, local copies, waits for them, and re-layouts  5.05 us

profile of v2, /device:TPU:39, one launch (start us, length us, event | category | flops | bytes accessed | tf_op | source)
XLA Modules:
  0.0 42.3 jit_solution(4985663719855014760)
XLA Ops:
  0.6 0.0 copy-start
  0.6 0.9 %copy-done = f32[9,32,32]{2,1,0:T(8,128)S(1)} copy-done((f32[9,32,32]{2,1,0:T(8,128)S(1)}, f32[9,32,32]{2,1,0:T(8,128)}, u32[]{:S(2)}) %copy-start) | copy-done | bytes 36888
  1.5 36.6 %shard_map.41 = (f32[25,32,32]{2,1,0:T(8,128)S(1)}, f32[32,32,2048]{2,1,0:T(8,128)S(1)}) custom-call(f32[9,32,32]{2,1,0:T(8,128)S(1)} %copy-done, f32[32,32,2048]{2,1,0:T(8,128)} %v_hbm.1), custom_call_target="tpu_custom_call" | custom-call | tf_op jit(solution)/shard_map/pallas_call | solution.py:365
  38.1 0.8 %copy.6 = f32[25,32,32]{2,1,0:T(8,128)} copy(f32[25,32,32]{2,1,0:T(8,128)S(1)} %get-tuple-element.2) | data formatting | bytes 204800
  38.9 3.4 %copy.7 = f32[32,32,2048]{2,1,0:T(8,128)} copy(f32[32,32,2048]{2,1,0:T(8,128)S(1)} %get-tuple-element.3) | data formatting | bytes 16777216
Async XLA Ops:
  0.6 0.9 %copy-start = (f32[9,32,32]{2,1,0:T(8,128)S(1)}, f32[9,32,32]{2,1,0:T(8,128)}, u32[]{:S(2)}) copy-start(f32[9,32,32]{2,1,0:T(8,128)} %coef_hbm.1) | copy-start | bytes 110596

commit v3 on v2

--- a/solution.py
+++ b/solution.py
@@ -13,6 +13,9 @@
 STEPS = ((-1, 0), (1, 0), (0, -1), (0, 1), (-1, -1), (-1, 1), (1, -1), (1, 1))
 UP, DOWN, LEFT, RIGHT = 0, 1, 2, 3
 CHUNKS = 8
+GROUP = 4
+SETS = 3
+LEFT_OVER = 2
 SLOTS = [((m // 3 - k // 3) + 2) * 5 + (m % 3 - k % 3) + 2 for k in range(9) for m in range(9)]
 
 
@@ -22,13 +25,12 @@
 
 def kernel(
     rows_total, cols_total,
-    coef_hbm, v_hbm, normal_ref, image_ref,
+    coef_hbm, v_hbm, normal_ref, image_ref, t_hi, t_lo, w_hi, w_lo,
     coef, padded, flipped, shifted, nts,
-    v_vm, up_vm, down_vm, col_vm, col_out, corner_out, relay_vm,
+    v_vm, up_vm, down_vm, col_vm, col_out, corner_out, relay_vm, hop_vm, diag_out, diag_vm,
     row_msg, col_msg, heard,
-    t_hi, t_lo, w_hi, w_lo,
     load_sem, coef_sem, msg_send, msg_recv, row_send, row_recv, col_send, col_recv, cor_send, cor_recv,
-    relay_recv, relay_send,
+    relay_recv, relay_send, hop_recv, hop_send, diag_send, diag_recv,
 ):
     gy = lax.axis_index("gy")
     gx = lax.axis_index("gx")
@@ -48,21 +50,59 @@
     def lanes(i):
         return pl.ds(pl.multiple_of(i * width, width), width)
 
-    def load(i):
-        return pltpu.make_async_copy(v_hbm.at[:, :, lanes(i)], v_vm.at[:, :, lanes(i)], load_sem.at[i])
+    def span(n):
+        return pl.ds(0, n * width)
+
+    def load(part):
+        return pltpu.make_async_copy(v_hbm.at[part], v_vm.at[part], load_sem)
 
     def row_copy(s, i):
         src = v_hbm.at[0:2, :, lanes(i)] if s == UP else v_hbm.at[rows - 2:rows, :, lanes(i)]
         dst = down_vm if s == UP else up_vm
         return pltpu.make_async_remote_copy(
-            src_ref=src, dst_ref=dst.at[:, :, lanes(i)], send_sem=row_send.at[s, i],
+            src_ref=src, dst_ref=dst.at[:, :, lanes(i)], send_sem=row_send.at[s],
             recv_sem=row_recv.at[s, i], device_id=at(s), device_id_type=MESH)
+
+    odd = gy % 2 == 1
+    plane = gy // 2
+    crossing = (jnp.logical_not(odd), odd)
+    late = jnp.where(odd, 2 * plane + 2, CHUNKS - 2 * plane)
+    held = jnp.where(odd, 2 * plane, jnp.maximum(CHUNKS - 2 - 2 * plane, 0))
+
+    def hop(s, i, count):
+        src = v_hbm.at[0:2, :, lanes(i)] if s == UP else v_hbm.at[rows - 2:rows, :, lanes(i)]
+        slot = i - CHUNKS + count
+        return pltpu.make_async_remote_copy(
+            src_ref=src, dst_ref=hop_vm.at[slot], send_sem=row_send.at[s], recv_sem=hop_recv.at[slot],
+            device_id=(gy + (2 if s == DOWN else -2), gx), device_id_type=MESH)
+
+    def send_rows(i):
+        for s in (UP, DOWN):
+            detoured = crossing[s] & (i >= CHUNKS - late)
+            when(exists(s) & jnp.logical_not(detoured), lambda s=s: row_copy(s, i).start())
+            when(exists(s) & detoured, lambda s=s: hop(s, i, late).start())
+
+    def hop_on(s, slot):
+        i = CHUNKS - held + slot
+        return pltpu.make_async_remote_copy(
+            src_ref=hop_vm.at[slot], dst_ref=(down_vm if s == UP else up_vm).at[:, :, lanes(i)],
+            send_sem=hop_send.at[slot], recv_sem=row_recv.at[s, i],
+            device_id=(gy + (1 if s == UP else -1), gx), device_id_type=MESH)
+
+    def each_held(slots, f):
+        for s in (UP, DOWN):
+            for slot in slots:
+                when(crossing[s] & (slot < held), functools.partial(f, s, slot))
+
+    def hop_pass(s, slot):
+        hop(s, CHUNKS - held + slot, held).wait_recv()
+        hop_on(s, slot).start()
 
     def col_copy(s, i):
         j = 2 - 2 * s
         return pltpu.make_async_remote_copy(
             src_ref=col_out.at[s, :, :, lanes(i)], dst_ref=col_vm.at[j:j + 2, 0:rows, lanes(i)],
-            send_sem=col_send.at[s, i], recv_sem=col_recv.at[s, i], device_id=at(LEFT + s), device_id_type=MESH)
+            send_sem=col_send.at[s], recv_sem=col_recv.at[s, i // GROUP], device_id=at(LEFT + s), device_id_type=MESH)
 
     turns = ((gx == TURN + 1), (gx == TURN))
 
@@ -71,7 +111,7 @@
         via = jnp.where(i % 3 == 0, first, second)
         return pltpu.make_async_remote_copy(
             src_ref=col_out.at[s, :, :, lanes(i)], dst_ref=relay_vm.at[i // 3],
-            send_sem=col_send.at[s, i], recv_sem=relay_recv.at[i // 3], device_id=(gy, via), device_id_type=MESH)
+            send_sem=col_send.at[s], recv_sem=relay_recv.at[i // 3], device_id=(gy, via), device_id_type=MESH)
 
     def send_cols(s, i):
         around = turns[s] & (i % 3 < 2)
@@ -82,7 +122,7 @@
         j = 2 - 2 * s
         return pltpu.make_async_remote_copy(
             src_ref=relay_vm.at[i // 3], dst_ref=col_vm.at[j:j + 2, 0:rows, lanes(i)],
-            send_sem=relay_send.at[i // 3], recv_sem=col_recv.at[s, i], device_id=(gy, TURN + s), device_id_type=MESH)
+            send_sem=relay_send.at[i // 3], recv_sem=col_recv.at[s, i // GROUP], device_id=(gy, TURN + s), device_id_type=MESH)
 
     def relays(f):
         for s in (0, 1):
@@ -108,14 +148,19 @@
         j = 2 - 2 * s
         return pltpu.make_async_remote_copy(
             src_ref=corner_out.at[s, :, :, lanes(i)], dst_ref=col_vm.at[j:j + 2, rows:rows + 8, lanes(i)],
-            send_sem=cor_send.at[s, i], recv_sem=cor_recv.at[s, i], device_id=at(LEFT + s), device_id_type=MESH)
+            send_sem=cor_send.at[s], recv_sem=cor_recv.at[s, i], device_id=at(LEFT + s), device_id_type=MESH)
 
     def msg_copy(n):
         dy, dx = STEPS[n]
         src = row_msg.at[(dy + 1) // 2] if dy else col_msg.at[(dx + 1) // 2]
         return pltpu.make_async_remote_copy(
-            src_ref=src, dst_ref=heard.at[n], send_sem=msg_send.at[n], recv_sem=msg_recv.at[n],
+            src_ref=src, dst_ref=heard.at[n], send_sem=msg_send, recv_sem=msg_recv,
             device_id=at(n), device_id_type=MESH)
+
+    def diag_copy(n):
+        return pltpu.make_async_remote_copy(
+            src_ref=diag_out.at[n - 4], dst_ref=diag_vm.at[n - 4], send_sem=diag_send.at[n - 4],
+            recv_sem=diag_recv.at[n - 4], device_id=at(n), device_id_type=MESH)
 
     opposite = [STEPS.index((-dy, -dx)) for dy, dx in STEPS]
 
@@ -123,33 +168,29 @@
         pl.when(pred)(f)
 
     take_coef = pltpu.make_async_copy(coef_hbm, coef, coef_sem)
+    barrier = pltpu.get_barrier_semaphore()
     take_coef.start()
-    for i in range(CHUNKS):
-        load(i).start()
-
-    barrier = pltpu.get_barrier_semaphore()
     known = jnp.int32(0)
     for n in range(8):
         when(exists(n), lambda n=n: pl.semaphore_signal(barrier, inc=1, device_id=at(n), device_id_type=MESH))
         known = known + exists(n).astype(jnp.int32)
+    for dy in (-2, 2):
+        there = (gy + dy >= 0) & (gy + dy < ny)
+        when(there, lambda dy=dy: pl.semaphore_signal(barrier, inc=1, device_id=(gy + dy, gx), device_id_type=MESH))
+        known = known + there.astype(jnp.int32)
     for side in RELAYS:
         for via in side:
             for end in (TURN, TURN + 1):
                 for me, other in ((via, end), (end, via)):
                     when(gx == me, lambda other=other: pl.semaphore_signal(barrier, inc=1, device_id=(gy, other), device_id_type=MESH))
                     known = known + (gx == me).astype(jnp.int32)
-    pl.semaphore_wait(barrier, known)
-
-    def send_rows(i):
-        for s in (UP, DOWN):
-            when(exists(s), lambda s=s: row_copy(s, i).start())
-
-    send_rows(0)
     padded[...] = jnp.zeros_like(padded)
     row_msg[...] = jnp.zeros_like(row_msg)
     col_msg[...] = jnp.zeros_like(col_msg)
     flipped[...] = jnp.zeros_like(flipped)
     take_coef.wait()
+    for q in range(4):
+        load(pl.ds(8 * q, 8)).start()
     padded[0:9, :, 0:cols] = coef[...]
     lane = lax.broadcasted_iota(jnp.int32, (8, 128), 1)
     for e, r in ((0, 0), (1, rows - 1)):
@@ -162,6 +203,8 @@
         col_msg[0, g:g + 1, :] = turned[0:1]
         col_msg[1, g:g + 1, :] = turned[cols - 1:cols]
         flipped[g, 1:cols + 1, :] = turned[0:cols]
+    pl.semaphore_wait(barrier, known)
+
     for n in range(8):
         when(exists(n), lambda n=n: msg_copy(n).start())
 
@@ -169,7 +212,7 @@
         send_rows(i)
         return c
 
-    lax.fori_loop(1, CHUNKS, rest, 0)
+    lax.fori_loop(0, CHUNKS, rest, 0)
 
     corner_out[...] = jnp.zeros_like(corner_out)
 
@@ -182,7 +225,6 @@
     when(jnp.logical_not(exists(RIGHT)), lambda: clear(col_vm.at[2:4]))
 
     def pack(i, c):
-        load(i).wait()
         for s in (0, 1):
             for j in (0, 1):
                 col = j if s == 0 else cols - 2 + j
@@ -192,10 +234,29 @@
             send_cols(s, i)
         return c
 
+    load(pl.ds(0, rows)).wait()
     lax.fori_loop(0, CHUNKS, pack, 0)
-
+    for n in range(4, 8):
+        dy, dx = STEPS[n]
+        for c in (0, 1):
+            for h in (0, 1):
+                row, col = (h if dy < 0 else rows - 2 + h), (c if dx < 0 else cols - 2 + c)
+                diag_out[n - 4, 2 * c + h:2 * c + h + 1, :] = v_vm[row, col:col + 1, lanes(CHUNKS - 1)]
+        when(exists(n), lambda n=n: diag_copy(n).start())
+        when(jnp.logical_not(exists(opposite[n])), lambda n=n: clear(diag_vm.at[n - 4]))
+
+    def sent(ref, sem):
+        pltpu.make_async_copy(ref, ref, sem).wait()
+
+    neighbours = jnp.int32(0)
     for n in range(8):
-        when(exists(opposite[n]), lambda n=n: msg_copy(n).wait_recv())
+        neighbours = neighbours + exists(n).astype(jnp.int32)
+
+    def messages(sem):
+        for n in (3, 5, 8):
+            when(neighbours == n, lambda n=n: sent(heard.at[0:n], sem))
+
+    messages(msg_recv)
 
     def from_side(n):
         return heard[opposite[n]]
@@ -286,49 +347,73 @@
                 t_lo[b, rl * 32:rl * 32 + 32, tile * 128:tile * 128 + 128] = (x - hi.astype(F32)).astype(BF16)
         return c
 
+    lax.fori_loop(0, 2, build, 0)
     pass_on(0)
-    lax.fori_loop(0, 2, build, 0)
+    each_held((0, 1), hop_pass)
+    lax.fori_loop(2, 4, build, 0)
     pass_on(1)
-    lax.fori_loop(2, 4, build, 0)
-    pass_on(2)
+    each_held((2,), hop_pass)
 
     def halves(x):
         hi = x.astype(BF16)
         return hi, (x - hi.astype(F32)).astype(BF16)
 
-    def put(block, start, hi, lo):
-        w_hi[block, start:start + hi.shape[0], :] = hi
-        w_lo[block, start:start + hi.shape[0], :] = lo
+    def put(i, block, start, hi, lo):
+        w_hi[i % SETS, block, start:start + hi.shape[0], :] = hi
+        w_lo[i % SETS, block, start:start + hi.shape[0], :] = lo
+
+    def own_part(i):
+        for q in range(4):
+            hi, lo = halves(v_vm[8 * q:8 * q + 8, :, lanes(i)].reshape(256, width))
+            put(i, q, 64, hi, lo)
+            if q > 0:
+                put(i, q - 1, 320, hi[0:64], lo[0:64])
+            if q < 3:
+                put(i, q + 1, 0, hi[192:256], lo[192:256])
+
+    def side_part(i, last=False):
+        def columns(s):
+            j = 2 - 2 * s
+            at_group = pl.ds(pl.multiple_of(i * width, width), GROUP * width)
+            whole = col_vm.at[j:j + 2, 0:rows, at_group]
+            pltpu.make_async_copy(whole, whole, col_recv.at[s, i // GROUP]).wait()
+
+        for s in (0, 1):
+            if not last:
+                when(exists(LEFT + 1 - s) & (i % GROUP == 0), functools.partial(columns, s))
+                when(exists(LEFT + 1 - s), lambda s=s: cor_copy(s, i).wait_recv())
+        if last:
+            for n in range(4, 8):
+                when(exists(opposite[n]), lambda n=n: diag_copy(n).wait_recv())
+        for j in range(4):
+            hi, lo = halves(col_vm[j, 0:32, lanes(i)])
+            if last:
+                from_above, from_below = (6, 4) if j >= 2 else (7, 5)
+                c = 2 * (j % 2)
+                corner = jnp.concatenate([
+                    diag_vm[from_above - 4, c:c + 2, :], diag_vm[from_below - 4, c:c + 2, :], jnp.zeros((12, width), F32)], axis=0)
+            else:
+                corner = jnp.concatenate([col_vm[j, 32:40, lanes(i)], jnp.zeros((8, width), F32)], axis=0)
+            chi, clo = halves(corner)
+            put(i, 0, 384 + 32 * j, hi[0:16], lo[0:16])
+            put(i, 0, 400 + 32 * j, chi, clo)
+            put(i, 1, 384 + 32 * j, hi, lo)
+            put(i, 2, 384 + 32 * j, hi, lo)
+            put(i, 3, 384 + 32 * j, hi[16:32], lo[16:32])
+            put(i, 3, 400 + 32 * j, chi, clo)
 
     def compute(i):
-        at_i = lanes(i)
-        for s in (0, 1):
-            when(exists(LEFT + 1 - s), lambda s=s: (col_copy(s, i).wait_recv(), cor_copy(s, i).wait_recv())[0])
+        side_part(i)
         for q in range(4):
-            hi, lo = halves(v_vm[8 * q:8 * q + 8, :, at_i].reshape(256, width))
-            put(q, 64, hi, lo)
-            if q > 0:
-                put(q - 1, 320, hi[0:64], lo[0:64])
-            if q < 3:
-                put(q + 1, 0, hi[192:256], lo[192:256])
-        put(0, 0, *halves(up_vm[:, :, at_i].reshape(64, width)))
-        put(3, 320, *halves(down_vm[:, :, at_i].reshape(64, width)))
-        for j in range(4):
-            hi, lo = halves(col_vm[j, 0:32, at_i])
-            chi, clo = halves(jnp.concatenate([col_vm[j, 32:40, at_i], jnp.zeros((8, width), F32)], axis=0))
-            put(0, 384 + 32 * j, hi[0:16], lo[0:16])
-            put(0, 400 + 32 * j, chi, clo)
-            put(1, 384 + 32 * j, hi, lo)
-            put(2, 384 + 32 * j, hi, lo)
-            put(3, 384 + 32 * j, hi[16:32], lo[16:32])
-            put(3, 400 + 32 * j, chi, clo)
-        for q in range(4):
-            y = jnp.dot(t_hi[q], w_hi[q], preferred_element_type=F32)
-            y = y + jnp.dot(t_lo[q], w_hi[q], preferred_element_type=F32)
-            y = y + jnp.dot(t_hi[q], w_lo[q], preferred_element_type=F32)
-            image_ref[8 * q:8 * q + 8, :, at_i] = y.reshape(8, cols, width)
+            y = products(t_hi[q], t_lo[q], w_hi[i % SETS, q], w_lo[i % SETS, q])
+            image_ref[8 * q:8 * q + 8, :, lanes(i)] = y.reshape(8, cols, width)
 
     def main(i, c):
+        for step, slots in ((1, (3,)), (2, (4,)), (3, (5,))):
+            when(i == step, lambda slots=slots: each_held(slots, hop_pass))
+        when(i == 2, lambda: pass_on(2))
+        own_part(i)
+        when(i > 1, lambda: compute(i - 2))
         for s in (UP, DOWN):
             when(exists(1 - s), lambda s=s: row_copy(s, i).wait_recv())
         for s in (0, 1):
@@ -337,24 +422,52 @@
                 for h in (0, 1):
                     corner_out[s, j, h:h + 1, lanes(i)] = up_vm[h, col:col + 1, lanes(i)]
                     corner_out[s, j, 2 + h:3 + h, lanes(i)] = down_vm[h, col:col + 1, lanes(i)]
-            when(exists(LEFT + s), lambda s=s: cor_copy(s, i).start())
-        when(i > 0, lambda: compute(i - 1))
+            when(exists(LEFT + s) & (i < CHUNKS - 1), lambda s=s: cor_copy(s, i).start())
+        put(i, 0, 0, *halves(up_vm[:, :, lanes(i)].reshape(64, width)))
+        put(i, 3, 320, *halves(down_vm[:, :, lanes(i)].reshape(64, width)))
         return c
 
     lax.fori_loop(0, CHUNKS, main, 0)
-    compute(CHUNKS - 1)
-
-    def finish(i, c):
-        for s in (0, 1):
-            when(exists(s), lambda s=s: row_copy(s, i).wait_send())
-            when(exists(LEFT + s), lambda s=s: (col_copy(s, i).wait_send(), cor_copy(s, i).wait_send())[0])
-        return c
-
-    lax.fori_loop(0, CHUNKS, finish, 0)
-    for n in range(8):
-        when(exists(n), lambda n=n: msg_copy(n).wait_send())
+    side_part(CHUNKS - 2)
+    side_part(CHUNKS - 1, last=True)
+
+    for s in (0, 1):
+        when(exists(s), lambda s=s: sent(up_vm, row_send.at[s]))
+        when(exists(LEFT + s), lambda s=s: sent(col_out.at[s], col_send.at[s]))
+        when(exists(LEFT + s), lambda s=s: sent(corner_out.at[s, :, :, span(CHUNKS - 1)], cor_send.at[s]))
+    for n in range(4, 8):
+        when(exists(n), lambda n=n: diag_copy(n).wait_send())
+    messages(msg_send)
     for j in range(3):
         passed_on(j)
+    each_held(range(6), lambda s, slot: hop_on(s, slot).wait_send())
+
+
+def products(t_hi, t_lo, w_hi, w_lo):
+    y = jnp.dot(t_hi, w_hi, preferred_element_type=F32)
+    y = y + jnp.dot(t_lo, w_hi, preferred_element_type=F32)
+    return y + jnp.dot(t_hi, w_lo, preferred_element_type=F32)
+
+
+def last_chunks(normal_vm, image_vm, t_hi, t_lo, w_hi, w_lo, normal_hbm, image_hbm, tail, normal_sem, image_sem, tail_sem):
+    rows, cols, nv = image_hbm.shape
+    width = nv // CHUNKS
+    done = nv - LEFT_OVER * width
+    copies = [pltpu.make_async_copy(
+        image_vm.at[8 * q:8 * q + 8, :, :], image_hbm.at[8 * q:8 * q + 8, :, 0:done], image_sem.at[q]) for q in range(4)]
+    copies.append(pltpu.make_async_copy(normal_vm, normal_hbm, normal_sem))
+    for copy in copies:
+        copy.start()
+    for n in range(LEFT_OVER):
+        i = CHUNKS - LEFT_OVER + n
+        for q in range(4):
+            y = products(t_hi[q], t_lo[q], w_hi[i % SETS, q], w_lo[i % SETS, q])
+            tail[n, q] = y.reshape(8, cols, width)
+            copies.append(pltpu.make_async_copy(
+                tail.at[n, q], image_hbm.at[8 * q:8 * q + 8, :, i * width:i * width + width], tail_sem.at[n, q]))
+            copies[-1].start()
+    for copy in copies:
+        copy.wait()
 
 
 def per_device(rows_total, cols_total, coefficients, vectors):
@@ -362,11 +475,14 @@
     nv = vectors.shape[2]
     width = nv // CHUNKS
     dma = pltpu.SemaphoreType.DMA
-    return pl.pallas_call(
+    parts = pl.pallas_call(
         functools.partial(kernel, rows_total, cols_total),
-        out_shape=(pltpu.VMEM((25, rows, cols), F32), pltpu.VMEM((rows, cols, nv), F32)),
+        out_shape=(
+            pltpu.VMEM((25, rows, cols), F32), pltpu.VMEM((rows, cols, nv - LEFT_OVER * width), F32),
+            pltpu.VMEM((4, 256, 512), BF16), pltpu.VMEM((4, 256, 512), BF16),
+            pltpu.VMEM((SETS, 4, 512, width), BF16), pltpu.VMEM((SETS, 4, 512, width), BF16)),
         in_specs=[pl.BlockSpec(memory_space=pltpu.HBM)] * 2,
-        out_specs=(pl.BlockSpec(memory_space=pltpu.VMEM),) * 2,
+        out_specs=(pl.BlockSpec(memory_space=pltpu.VMEM),) * 6,
         scratch_shapes=[
             pltpu.VMEM((9, rows, cols), F32),
             pltpu.VMEM((12, rows, 128), F32),
@@ -380,22 +496,31 @@
             pltpu.VMEM((2, 2, rows, nv), F32),
             pltpu.VMEM((2, 2, 8, nv), F32),
             pltpu.VMEM((3, 2, rows, width), F32),
+            pltpu.VMEM((6, 2, cols, width), F32),
+            pltpu.VMEM((4, 4, width), F32),
+            pltpu.VMEM((4, 4, width), F32),
             pltpu.VMEM((2, 8, 128), F32),
             pltpu.VMEM((2, 8, 128), F32),
             pltpu.VMEM((8, 8, 128), F32),
-            pltpu.VMEM((4, 256, 512), BF16),
-            pltpu.VMEM((4, 256, 512), BF16),
-            pltpu.VMEM((4, 512, width), BF16),
-            pltpu.VMEM((4, 512, width), BF16),
-            dma((CHUNKS,)), dma,
-            dma((8,)), dma((8,)),
-            dma((2, CHUNKS)), dma((2, CHUNKS)),
-            dma((2, CHUNKS)), dma((2, CHUNKS)),
-            dma((2, CHUNKS)), dma((2, CHUNKS)),
+            dma, dma,
+            dma, dma,
+            dma((2,)), dma((2, CHUNKS)),
+            dma((2,)), dma((2, CHUNKS // GROUP)),
+            dma((2,)), dma((2, CHUNKS - 1)),
             dma((3,)), dma((3,)),
+            dma((6,)), dma((6,)),
+            dma((4,)), dma((4,)),
         ],
         compiler_params=pltpu.CompilerParams(collective_id=0, has_side_effects=True, vmem_limit_bytes=44 * 2**20),
-    )(coefficients, vectors)
+    )(pltpu.with_memory_space_constraint(coefficients, pltpu.HBM), vectors)
+    return pl.pallas_call(
+        last_chunks,
+        out_shape=(jax.ShapeDtypeStruct((25, rows, cols), F32), jax.ShapeDtypeStruct((rows, cols, nv), F32)),
+        in_specs=[pl.BlockSpec(memory_space=pltpu.VMEM)] * 6,
+        out_specs=(pl.BlockSpec(memory_space=pltpu.HBM),) * 2,
+        scratch_shapes=[pltpu.VMEM((LEFT_OVER, 4, 8, cols, width), F32), dma, dma((4,)), dma((LEFT_OVER, 4))],
+        compiler_params=pltpu.CompilerParams(vmem_limit_bytes=8 * 2**20),
+    )(*parts)
 
 
 def solution(mesh):

time: 43 us -> 37.5 us (0.87)
  the two profiles are of different devices: /device:TPU:39 before, /device:TPU:103 now
where the time goes in v3:
time: 37.5 us; the launch traced here: 37.4 us
  Pallas kernels  36.8 us (98%)
  between operations  0.64 us (2%)
    pallas_call x1, Pallas kernels, per_device(): pl.pallas_call(functools.partial(kernel, rows_total, cols_total), out_sha...  33.2 us
    pallas_call x1, Pallas kernels, per_device(): pl.pallas_call(last_chunks, out_shape=(jax.ShapeDtypeStruct((25, rows, co...  3.54 us

profile of v3, /device:TPU:103, one launch (start us, length us, event | category | flops | bytes accessed | tf_op | source)
XLA Modules:
  0.0 37.4 jit_solution(8594019029691088145)
XLA Ops:
  0.6 33.2 %shard_map.41 = (f32[25,32,32]{2,1,0:T(8,128)S(1)}, f32[32,32,1536]{2,1,0:T(8,128)S(1)}, bf16[4,256,512]{2,1,0:T(8,128)(2,1)S(1)}, bf16[4,256,512]{2,1,0:T(8,128...) custom-call(f32[9,32,32]{2,1,0:T(8,128)} %coef_hbm.1, f32[32,32,2048]{2,1,0:T(8,128)} %v_hbm.1), custom_call_target="tpu_custom_call" | custom-call | tf_op jit(solution)/shard_map/pallas_call | solution.py:478
  33.9 3.5 %shard_map.42 = (f32[25,32,32]{2,1,0:T(8,128)}, f32[32,32,2048]{2,1,0:T(8,128)}) custom-call(f32[25,32,32]{2,1,0:T(8,128)S(1)} %get-tuple-element.8.normal_vm, f32[32,32,1536]{2,1,0:T(8,128)S(1)} %get-tuple-element.9.image_vm, bf16[4,256,512]{2,1,0:T(8,128)(2,1)S(1)} %get-tuple-element.10.t_hi, bf16[4,256,512]{2,1,0:T(8,128)(2,1)S(1)} %get-tuple-element.11.t_lo, ...), custom_call_target="tpu_custom_call" | custom-call | tf_op jit(solution)/shard_map/pallas_call | solution.py:516

commit v4 on v3

--- a/solution.py
+++ b/solution.py
@@ -14,8 +14,8 @@
 UP, DOWN, LEFT, RIGHT = 0, 1, 2, 3
 CHUNKS = 8
 GROUP = 4
-SETS = 3
-LEFT_OVER = 2
+LAG = 3
+SETS = LAG + 1
 SLOTS = [((m // 3 - k // 3) + 2) * 5 + (m % 3 - k % 3) + 2 for k in range(9) for m in range(9)]
 
 
@@ -27,7 +27,7 @@
     rows_total, cols_total,
     coef_hbm, v_hbm, normal_ref, image_ref, t_hi, t_lo, w_hi, w_lo,
     coef, padded, flipped, shifted, nts,
-    v_vm, up_vm, down_vm, col_vm, col_out, corner_out, relay_vm, hop_vm, diag_out, diag_vm,
+    v_vm, up_vm, down_vm, col_vm, col_out, corner_out, corner_vm, relay_vm, hop_vm, diag_out, diag_vm,
     row_msg, col_msg, heard,
     load_sem, coef_sem, msg_send, msg_recv, row_send, row_recv, col_send, col_recv, cor_send, cor_recv,
     relay_recv, relay_send, hop_recv, hop_send, diag_send, diag_recv,
@@ -145,9 +145,8 @@
         relays(one)
 
     def cor_copy(s, i):
-        j = 2 - 2 * s
-        return pltpu.make_async_remote_copy(
-            src_ref=corner_out.at[s, :, :, lanes(i)], dst_ref=col_vm.at[j:j + 2, rows:rows + 8, lanes(i)],
+        return pltpu.make_async_remote_copy(
+            src_ref=corner_out.at[s, :, lanes(i)], dst_ref=corner_vm.at[s, :, lanes(i)],
             send_sem=cor_send.at[s], recv_sem=cor_recv.at[s, i], device_id=at(LEFT + s), device_id_type=MESH)
 
     def msg_copy(n):
@@ -214,15 +213,14 @@
 
     lax.fori_loop(0, CHUNKS, rest, 0)
 
-    corner_out[...] = jnp.zeros_like(corner_out)
-
     def clear(ref):
         ref[...] = jnp.zeros_like(ref)
 
     when(jnp.logical_not(exists(UP)), lambda: clear(up_vm))
     when(jnp.logical_not(exists(DOWN)), lambda: clear(down_vm))
-    when(jnp.logical_not(exists(LEFT)), lambda: clear(col_vm.at[0:2]))
-    when(jnp.logical_not(exists(RIGHT)), lambda: clear(col_vm.at[2:4]))
+    for s in (0, 1):
+        j = 2 - 2 * s
+        when(jnp.logical_not(exists(LEFT + 1 - s)), lambda s=s, j=j: (clear(col_vm.at[j:j + 2]), clear(corner_vm.at[s]))[0])
 
     def pack(i, c):
         for s in (0, 1):
@@ -393,7 +391,8 @@
                 corner = jnp.concatenate([
                     diag_vm[from_above - 4, c:c + 2, :], diag_vm[from_below - 4, c:c + 2, :], jnp.zeros((12, width), F32)], axis=0)
             else:
-                corner = jnp.concatenate([col_vm[j, 32:40, lanes(i)], jnp.zeros((8, width), F32)], axis=0)
+                c = 4 * (j % 2)
+                corner = jnp.concatenate([corner_vm[1 - j // 2, c:c + 4, lanes(i)], jnp.zeros((12, width), F32)], axis=0)
             chi, clo = halves(corner)
             put(i, 0, 384 + 32 * j, hi[0:16], lo[0:16])
             put(i, 0, 400 + 32 * j, chi, clo)
@@ -413,28 +412,29 @@
             when(i == step, lambda slots=slots: each_held(slots, hop_pass))
         when(i == 2, lambda: pass_on(2))
         own_part(i)
-        when(i > 1, lambda: compute(i - 2))
+        when(i >= LAG, lambda: compute(i - LAG))
         for s in (UP, DOWN):
             when(exists(1 - s), lambda s=s: row_copy(s, i).wait_recv())
         for s in (0, 1):
             for j in (0, 1):
                 col = j if s == 0 else cols - 2 + j
                 for h in (0, 1):
-                    corner_out[s, j, h:h + 1, lanes(i)] = up_vm[h, col:col + 1, lanes(i)]
-                    corner_out[s, j, 2 + h:3 + h, lanes(i)] = down_vm[h, col:col + 1, lanes(i)]
+                    corner_out[s, 4 * j + h:4 * j + h + 1, lanes(i)] = up_vm[h, col:col + 1, lanes(i)]
+                    corner_out[s, 4 * j + 2 + h:4 * j + 3 + h, lanes(i)] = down_vm[h, col:col + 1, lanes(i)]
             when(exists(LEFT + s) & (i < CHUNKS - 1), lambda s=s: cor_copy(s, i).start())
         put(i, 0, 0, *halves(up_vm[:, :, lanes(i)].reshape(64, width)))
         put(i, 3, 320, *halves(down_vm[:, :, lanes(i)].reshape(64, width)))
         return c
 
     lax.fori_loop(0, CHUNKS, main, 0)
-    side_part(CHUNKS - 2)
+    for i in range(CHUNKS - LAG, CHUNKS - 1):
+        side_part(i)
     side_part(CHUNKS - 1, last=True)
 
     for s in (0, 1):
         when(exists(s), lambda s=s: sent(up_vm, row_send.at[s]))
         when(exists(LEFT + s), lambda s=s: sent(col_out.at[s], col_send.at[s]))
-        when(exists(LEFT + s), lambda s=s: sent(corner_out.at[s, :, :, span(CHUNKS - 1)], cor_send.at[s]))
+        when(exists(LEFT + s), lambda s=s: sent(corner_out.at[s, :, span(CHUNKS - 1)], cor_send.at[s]))
     for n in range(4, 8):
         when(exists(n), lambda n=n: diag_copy(n).wait_send())
     messages(msg_send)
@@ -452,14 +452,14 @@
 def last_chunks(normal_vm, image_vm, t_hi, t_lo, w_hi, w_lo, normal_hbm, image_hbm, tail, normal_sem, image_sem, tail_sem):
     rows, cols, nv = image_hbm.shape
     width = nv // CHUNKS
-    done = nv - LEFT_OVER * width
+    done = nv - LAG * width
     copies = [pltpu.make_async_copy(
         image_vm.at[8 * q:8 * q + 8, :, :], image_hbm.at[8 * q:8 * q + 8, :, 0:done], image_sem.at[q]) for q in range(4)]
     copies.append(pltpu.make_async_copy(normal_vm, normal_hbm, normal_sem))
     for copy in copies:
         copy.start()
-    for n in range(LEFT_OVER):
-        i = CHUNKS - LEFT_OVER + n
+    for n in range(LAG):
+        i = CHUNKS - LAG + n
         for q in range(4):
             y = products(t_hi[q], t_lo[q], w_hi[i % SETS, q], w_lo[i % SETS, q])
             tail[n, q] = y.reshape(8, cols, width)
@@ -478,7 +478,7 @@
     parts = pl.pallas_call(
         functools.partial(kernel, rows_total, cols_total),
         out_shape=(
-            pltpu.VMEM((25, rows, cols), F32), pltpu.VMEM((rows, cols, nv - LEFT_OVER * width), F32),
+            pltpu.VMEM((25, rows, cols), F32), pltpu.VMEM((rows, cols, nv - LAG * width), F32),
             pltpu.VMEM((4, 256, 512), BF16), pltpu.VMEM((4, 256, 512), BF16),
             pltpu.VMEM((SETS, 4, 512, width), BF16), pltpu.VMEM((SETS, 4, 512, width), BF16)),
         in_specs=[pl.BlockSpec(memory_space=pltpu.HBM)] * 2,
@@ -492,9 +492,10 @@
             pltpu.VMEM((rows, cols, nv), F32),
             pltpu.VMEM((2, cols, nv), F32),
             pltpu.VMEM((2, cols, nv), F32),
-            pltpu.VMEM((4, rows + 8, nv), F32),
+            pltpu.VMEM((4, rows, nv), F32),
             pltpu.VMEM((2, 2, rows, nv), F32),
-            pltpu.VMEM((2, 2, 8, nv), F32),
+            pltpu.VMEM((2, 8, nv), F32),
+            pltpu.VMEM((2, 8, nv), F32),
             pltpu.VMEM((3, 2, rows, width), F32),
             pltpu.VMEM((6, 2, cols, width), F32),
             pltpu.VMEM((4, 4, width), F32),
@@ -518,7 +519,7 @@
         out_shape=(jax.ShapeDtypeStruct((25, rows, cols), F32), jax.ShapeDtypeStruct((rows, cols, nv), F32)),
         in_specs=[pl.BlockSpec(memory_space=pltpu.VMEM)] * 6,
         out_specs=(pl.BlockSpec(memory_space=pltpu.HBM),) * 2,
-        scratch_shapes=[pltpu.VMEM((LEFT_OVER, 4, 8, cols, width), F32), dma, dma((4,)), dma((LEFT_OVER, 4))],
+        scratch_shapes=[pltpu.VMEM((LAG, 4, 8, cols, width), F32), dma, dma((4,)), dma((LAG, 4))],
         compiler_params=pltpu.CompilerParams(vmem_limit_bytes=8 * 2**20),
     )(*parts)
 

time: 37.5 us -> 36.7 us (0.979)
  the two profiles are of different devices: /device:TPU:103 before, /device:TPU:1 now
where the time goes in v4:
time: 36.7 us; the launch traced here: 36.6 us
  Pallas kernels  36 us (98%)
  between operations  0.64 us (2%)
    pallas_call x1, Pallas kernels, per_device(): pl.pallas_call(functools.partial(kernel, rows_total, cols_total), out_sha...  32.4 us
    pallas_call x1, Pallas kernels, per_device(): pl.pallas_call(last_chunks, out_shape=(jax.ShapeDtypeStruct((25, rows, co...  3.56 us

profile of v4, /device:TPU:1, one launch (start us, length us, event | category | flops | bytes accessed | tf_op | source)
XLA Modules:
  0.0 36.6 jit_solution(11716925604995129635)
XLA Ops:
  0.6 32.4 %shard_map.41 = (f32[25,32,32]{2,1,0:T(8,128)S(1)}, f32[32,32,1280]{2,1,0:T(8,128)S(1)}, bf16[4,256,512]{2,1,0:T(8,128)(2,1)S(1)}, bf16[4,256,512]{2,1,0:T(8,128...) custom-call(f32[9,32,32]{2,1,0:T(8,128)} %coef_hbm.1, f32[32,32,2048]{2,1,0:T(8,128)} %v_hbm.1), custom_call_target="tpu_custom_call" | custom-call | tf_op jit(solution)/shard_map/pallas_call | solution.py:478
  33.0 3.6 %shard_map.42 = (f32[25,32,32]{2,1,0:T(8,128)}, f32[32,32,2048]{2,1,0:T(8,128)}) custom-call(f32[25,32,32]{2,1,0:T(8,128)S(1)} %get-tuple-element.8.normal_vm, f32[32,32,1280]{2,1,0:T(8,128)S(1)} %get-tuple-element.9.image_vm, bf16[4,256,512]{2,1,0:T(8,128)(2,1)S(1)} %get-tuple-element.10.t_hi, bf16[4,256,512]{2,1,0:T(8,128)(2,1)S(1)} %get-tuple-element.11.t_lo, ...), custom_call_target="tpu_custom_call" | custom-call | tf_op jit(solution)/shard_map/pallas_call | solution.py:517

commit v5 on v4

--- a/solution.py
+++ b/solution.py
@@ -16,6 +16,7 @@
 GROUP = 4
 LAG = 3
 SETS = LAG + 1
+NEAR = 2
 SLOTS = [((m // 3 - k // 3) + 2) * 5 + (m % 3 - k % 3) + 2 for k in range(9) for m in range(9)]
 
 
@@ -27,7 +28,7 @@
     rows_total, cols_total,
     coef_hbm, v_hbm, normal_ref, image_ref, t_hi, t_lo, w_hi, w_lo,
     coef, padded, flipped, shifted, nts,
-    v_vm, up_vm, down_vm, col_vm, col_out, corner_out, corner_vm, relay_vm, hop_vm, diag_out, diag_vm,
+    v_vm, row_vm, col_vm, col_out, corner_out, corner_vm, relay_vm, hop_vm, diag_out, diag_vm,
     row_msg, col_msg, heard,
     load_sem, coef_sem, msg_send, msg_recv, row_send, row_recv, col_send, col_recv, cor_send, cor_recv,
     relay_recv, relay_send, hop_recv, hop_send, diag_send, diag_recv,
@@ -50,6 +51,8 @@
     def lanes(i):
         return pl.ds(pl.multiple_of(i * width, width), width)
 
+    up_vm, down_vm = row_vm.at[0], row_vm.at[1]
+
     def span(n):
         return pl.ds(0, n * width)
 
@@ -61,12 +64,13 @@
         dst = down_vm if s == UP else up_vm
         return pltpu.make_async_remote_copy(
             src_ref=src, dst_ref=dst.at[:, :, lanes(i)], send_sem=row_send.at[s],
-            recv_sem=row_recv.at[s, i], device_id=at(s), device_id_type=MESH)
+            recv_sem=row_recv.at[i], device_id=at(s), device_id_type=MESH)
 
     odd = gy % 2 == 1
     plane = gy // 2
     crossing = (jnp.logical_not(odd), odd)
     late = jnp.where(odd, 2 * plane + 2, CHUNKS - 2 * plane)
+    relaying = jnp.where(odd, gy >= 2, gy < ny - 2)
     held = jnp.where(odd, 2 * plane, jnp.maximum(CHUNKS - 2 - 2 * plane, 0))
 
     def hop(s, i, count):
@@ -86,7 +90,7 @@
         i = CHUNKS - held + slot
         return pltpu.make_async_remote_copy(
             src_ref=hop_vm.at[slot], dst_ref=(down_vm if s == UP else up_vm).at[:, :, lanes(i)],
-            send_sem=hop_send.at[slot], recv_sem=row_recv.at[s, i],
+            send_sem=hop_send, recv_sem=row_recv.at[i],
             device_id=(gy + (1 if s == UP else -1), gx), device_id_type=MESH)
 
     def each_held(slots, f):
@@ -122,7 +126,7 @@
         j = 2 - 2 * s
         return pltpu.make_async_remote_copy(
             src_ref=relay_vm.at[i // 3], dst_ref=col_vm.at[j:j + 2, 0:rows, lanes(i)],
-            send_sem=relay_send.at[i // 3], recv_sem=col_recv.at[s, i // GROUP], device_id=(gy, TURN + s), device_id_type=MESH)
+            send_sem=relay_send, recv_sem=col_recv.at[s, i // GROUP], device_id=(gy, TURN + s), device_id_type=MESH)
 
     def relays(f):
         for s in (0, 1):
@@ -137,17 +141,10 @@
                 forward(s, i).start()
         relays(one)
 
-    def passed_on(j):
-        def one(s, n):
-            i = n + 3 * j
-            if i < CHUNKS:
-                forward(s, i).wait_send()
-        relays(one)
-
     def cor_copy(s, i):
         return pltpu.make_async_remote_copy(
             src_ref=corner_out.at[s, :, lanes(i)], dst_ref=corner_vm.at[s, :, lanes(i)],
-            send_sem=cor_send.at[s], recv_sem=cor_recv.at[s, i], device_id=at(LEFT + s), device_id_type=MESH)
+            send_sem=cor_send.at[s], recv_sem=cor_recv.at[i], device_id=at(LEFT + s), device_id_type=MESH)
 
     def msg_copy(n):
         dy, dx = STEPS[n]
@@ -158,8 +155,8 @@
 
     def diag_copy(n):
         return pltpu.make_async_remote_copy(
-            src_ref=diag_out.at[n - 4], dst_ref=diag_vm.at[n - 4], send_sem=diag_send.at[n - 4],
-            recv_sem=diag_recv.at[n - 4], device_id=at(n), device_id_type=MESH)
+            src_ref=diag_out.at[n - 4], dst_ref=diag_vm.at[n - 4], send_sem=diag_send,
+            recv_sem=diag_recv, device_id=at(n), device_id_type=MESH)
 
     opposite = [STEPS.index((-dy, -dx)) for dy, dx in STEPS]
 
@@ -239,7 +236,7 @@
         for c in (0, 1):
             for h in (0, 1):
                 row, col = (h if dy < 0 else rows - 2 + h), (c if dx < 0 else cols - 2 + c)
-                diag_out[n - 4, 2 * c + h:2 * c + h + 1, :] = v_vm[row, col:col + 1, lanes(CHUNKS - 1)]
+                diag_out[n - 4, 2 * c + h:2 * c + h + 1, :] = v_vm[row, col:col + 1, nv - NEAR * width:nv]
         when(exists(n), lambda n=n: diag_copy(n).start())
         when(jnp.logical_not(exists(opposite[n])), lambda n=n: clear(diag_vm.at[n - 4]))
 
@@ -253,6 +250,19 @@
     def messages(sem):
         for n in (3, 5, 8):
             when(neighbours == n, lambda n=n: sent(heard.at[0:n], sem))
+
+    corners = jnp.int32(0)
+    for n in range(4, 8):
+        corners = corners + exists(n).astype(jnp.int32)
+
+    def diagonals(sem):
+        for n in (1, 2, 4):
+            when(corners == n, lambda n=n: sent(diag_vm.at[0:n], sem))
+
+    def both_or_one(a, b, both, one, sem, i):
+        pair = exists(a) & exists(b)
+        when(pair, lambda: sent(both, sem.at[i]))
+        when(jnp.logical_not(pair), lambda: sent(one, sem.at[i]))
 
     messages(msg_recv)
 
@@ -369,27 +379,25 @@
             if q < 3:
                 put(i, q + 1, 0, hi[192:256], lo[192:256])
 
-    def side_part(i, last=False):
+    def side_part(i, near=None):
         def columns(s):
             j = 2 - 2 * s
             at_group = pl.ds(pl.multiple_of(i * width, width), GROUP * width)
             whole = col_vm.at[j:j + 2, 0:rows, at_group]
             pltpu.make_async_copy(whole, whole, col_recv.at[s, i // GROUP]).wait()
 
-        for s in (0, 1):
-            if not last:
+        if near is None:
+            for s in (0, 1):
                 when(exists(LEFT + 1 - s) & (i % GROUP == 0), functools.partial(columns, s))
-                when(exists(LEFT + 1 - s), lambda s=s: cor_copy(s, i).wait_recv())
-        if last:
-            for n in range(4, 8):
-                when(exists(opposite[n]), lambda n=n: diag_copy(n).wait_recv())
+            both_or_one(LEFT, RIGHT, corner_vm.at[:, :, lanes(i)], corner_vm.at[0, :, lanes(i)], cor_recv, i)
         for j in range(4):
             hi, lo = halves(col_vm[j, 0:32, lanes(i)])
-            if last:
+            if near is not None:
+                at_near = slice(near * width, near * width + width)
                 from_above, from_below = (6, 4) if j >= 2 else (7, 5)
                 c = 2 * (j % 2)
                 corner = jnp.concatenate([
-                    diag_vm[from_above - 4, c:c + 2, :], diag_vm[from_below - 4, c:c + 2, :], jnp.zeros((12, width), F32)], axis=0)
+                    diag_vm[from_above - 4, c:c + 2, at_near], diag_vm[from_below - 4, c:c + 2, at_near], jnp.zeros((12, width), F32)], axis=0)
             else:
                 c = 4 * (j % 2)
                 corner = jnp.concatenate([corner_vm[1 - j // 2, c:c + 4, lanes(i)], jnp.zeros((12, width), F32)], axis=0)
@@ -413,34 +421,36 @@
         when(i == 2, lambda: pass_on(2))
         own_part(i)
         when(i >= LAG, lambda: compute(i - LAG))
-        for s in (UP, DOWN):
-            when(exists(1 - s), lambda s=s: row_copy(s, i).wait_recv())
+        both_or_one(UP, DOWN, row_vm.at[:, :, :, lanes(i)], up_vm.at[:, :, lanes(i)], row_recv, i)
         for s in (0, 1):
             for j in (0, 1):
                 col = j if s == 0 else cols - 2 + j
                 for h in (0, 1):
                     corner_out[s, 4 * j + h:4 * j + h + 1, lanes(i)] = up_vm[h, col:col + 1, lanes(i)]
                     corner_out[s, 4 * j + 2 + h:4 * j + 3 + h, lanes(i)] = down_vm[h, col:col + 1, lanes(i)]
-            when(exists(LEFT + s) & (i < CHUNKS - 1), lambda s=s: cor_copy(s, i).start())
+            when(exists(LEFT + s) & (i < CHUNKS - NEAR), lambda s=s: cor_copy(s, i).start())
         put(i, 0, 0, *halves(up_vm[:, :, lanes(i)].reshape(64, width)))
         put(i, 3, 320, *halves(down_vm[:, :, lanes(i)].reshape(64, width)))
         return c
 
     lax.fori_loop(0, CHUNKS, main, 0)
-    for i in range(CHUNKS - LAG, CHUNKS - 1):
+    for i in range(CHUNKS - LAG, CHUNKS - NEAR):
         side_part(i)
-    side_part(CHUNKS - 1, last=True)
+    diagonals(diag_recv)
+    for near in range(NEAR):
+        side_part(CHUNKS - NEAR + near, near)
 
     for s in (0, 1):
         when(exists(s), lambda s=s: sent(up_vm, row_send.at[s]))
         when(exists(LEFT + s), lambda s=s: sent(col_out.at[s], col_send.at[s]))
-        when(exists(LEFT + s), lambda s=s: sent(corner_out.at[s, :, span(CHUNKS - 1)], cor_send.at[s]))
-    for n in range(4, 8):
-        when(exists(n), lambda n=n: diag_copy(n).wait_send())
+        when(exists(LEFT + s), lambda s=s: sent(corner_out.at[s, :, span(CHUNKS - NEAR)], cor_send.at[s]))
+    diagonals(diag_send)
     messages(msg_send)
-    for j in range(3):
-        passed_on(j)
-    each_held(range(6), lambda s, slot: hop_on(s, slot).wait_send())
+    for side in RELAYS:
+        for via in side:
+            when(gx == via, lambda: sent(relay_vm, relay_send))
+    for n in (2, 4, 6):
+        when(relaying & (held == n), lambda n=n: sent(hop_vm.at[0:n], hop_send))
 
 
 def products(t_hi, t_lo, w_hi, w_lo):
@@ -490,27 +500,26 @@
             pltpu.VMEM((3, 9, 40, 128), F32),
             pltpu.VMEM((4, 7, cols, 128), F32),
             pltpu.VMEM((rows, cols, nv), F32),
-            pltpu.VMEM((2, cols, nv), F32),
-            pltpu.VMEM((2, cols, nv), F32),
+            pltpu.VMEM((2, 2, cols, nv), F32),
             pltpu.VMEM((4, rows, nv), F32),
             pltpu.VMEM((2, 2, rows, nv), F32),
             pltpu.VMEM((2, 8, nv), F32),
             pltpu.VMEM((2, 8, nv), F32),
             pltpu.VMEM((3, 2, rows, width), F32),
             pltpu.VMEM((6, 2, cols, width), F32),
-            pltpu.VMEM((4, 4, width), F32),
-            pltpu.VMEM((4, 4, width), F32),
+            pltpu.VMEM((4, 4, NEAR * width), F32),
+            pltpu.VMEM((4, 4, NEAR * width), F32),
             pltpu.VMEM((2, 8, 128), F32),
             pltpu.VMEM((2, 8, 128), F32),
             pltpu.VMEM((8, 8, 128), F32),
             dma, dma,
             dma, dma,
-            dma((2,)), dma((2, CHUNKS)),
+            dma((2,)), dma((CHUNKS,)),
             dma((2,)), dma((2, CHUNKS // GROUP)),
-            dma((2,)), dma((2, CHUNKS - 1)),
-            dma((3,)), dma((3,)),
-            dma((6,)), dma((6,)),
-            dma((4,)), dma((4,)),
+            dma((2,)), dma((CHUNKS - NEAR,)),
+            dma((3,)), dma,
+            dma((6,)), dma,
+            dma, dma,
         ],
         compiler_params=pltpu.CompilerParams(collective_id=0, has_side_effects=True, vmem_limit_bytes=44 * 2**20),
     )(pltpu.with_memory_space_constraint(coefficients, pltpu.HBM), vectors)

time: 36.7 us -> 34.8 us (0.948)
  the two profiles are of different devices: /device:TPU:1 before, /device:TPU:43 now
where the time goes in v5:
time: 34.8 us; the launch traced here: 34.7 us
  Pallas kernels  34 us (98%)
  between operations  0.64 us (2%)
    pallas_call x1, Pallas kernels, per_device(): pl.pallas_call(functools.partial(kernel, rows_total, cols_total), out_sha...  30.5 us
    pallas_call x1, Pallas kernels, per_device(): pl.pallas_call(last_chunks, out_shape=(jax.ShapeDtypeStruct((25, rows, co...  3.56 us

profile of v5, /device:TPU:43, one launch (start us, length us, event | category | flops | bytes accessed | tf_op | source)
XLA Modules:
  0.0 34.7 jit_solution(3607133070485783751)
XLA Ops:
  0.6 30.5 %shard_map.41 = (f32[25,32,32]{2,1,0:T(8,128)S(1)}, f32[32,32,1280]{2,1,0:T(8,128)S(1)}, bf16[4,256,512]{2,1,0:T(8,128)(2,1)S(1)}, bf16[4,256,512]{2,1,0:T(8,128...) custom-call(f32[9,32,32]{2,1,0:T(8,128)} %coef_hbm.1, f32[32,32,2048]{2,1,0:T(8,128)} %v_hbm.1), custom_call_target="tpu_custom_call" | custom-call | tf_op jit(solution)/shard_map/pallas_call | solution.py:488
  31.1 3.6 %shard_map.42 = (f32[25,32,32]{2,1,0:T(8,128)}, f32[32,32,2048]{2,1,0:T(8,128)}) custom-call(f32[25,32,32]{2,1,0:T(8,128)S(1)} %get-tuple-element.8.normal_vm, f32[32,32,1280]{2,1,0:T(8,128)S(1)} %get-tuple-element.9.image_vm, bf16[4,256,512]{2,1,0:T(8,128)(2,1)S(1)} %get-tuple-element.10.t_hi, bf16[4,256,512]{2,1,0:T(8,128)(2,1)S(1)} %get-tuple-element.11.t_lo, ...), custom_call_target="tpu_custom_call" | custom-call | tf_op jit(solution)/shard_map/pallas_call | solution.py:526

commit v6 on v5

--- a/solution.py
+++ b/solution.py
@@ -20,7 +20,7 @@
 SLOTS = [((m // 3 - k // 3) + 2) * 5 + (m % 3 - k % 3) + 2 for k in range(9) for m in range(9)]
 
 
-RELAYS = (12, 11), (3, 4)
+RELAYS = (12, 11, 15), (3, 4, 0)
 TURN = 7
 
 
@@ -30,7 +30,7 @@
     coef, padded, flipped, shifted, nts,
     v_vm, row_vm, col_vm, col_out, corner_out, corner_vm, relay_vm, hop_vm, diag_out, diag_vm,
     row_msg, col_msg, heard,
-    load_sem, coef_sem, msg_send, msg_recv, row_send, row_recv, col_send, col_recv, cor_send, cor_recv,
+    load_sem, edge_sem, ready_sem, coef_sem, msg_send, msg_recv, row_send, row_recv, col_send, col_recv, cor_send, cor_recv,
     relay_recv, relay_send, hop_recv, hop_send, diag_send, diag_recv,
 ):
     gy = lax.axis_index("gy")
@@ -56,11 +56,12 @@
     def span(n):
         return pl.ds(0, n * width)
 
-    def load(part):
-        return pltpu.make_async_copy(v_hbm.at[part], v_vm.at[part], load_sem)
+    def load(first, count, sem):
+        part = pl.ds(first, count)
+        return pltpu.make_async_copy(v_hbm.at[part], v_vm.at[part], sem)
 
     def row_copy(s, i):
-        src = v_hbm.at[0:2, :, lanes(i)] if s == UP else v_hbm.at[rows - 2:rows, :, lanes(i)]
+        src = v_vm.at[0:2, :, lanes(i)] if s == UP else v_vm.at[rows - 2:rows, :, lanes(i)]
         dst = down_vm if s == UP else up_vm
         return pltpu.make_async_remote_copy(
             src_ref=src, dst_ref=dst.at[:, :, lanes(i)], send_sem=row_send.at[s],
@@ -74,7 +75,7 @@
     held = jnp.where(odd, 2 * plane, jnp.maximum(CHUNKS - 2 - 2 * plane, 0))
 
     def hop(s, i, count):
-        src = v_hbm.at[0:2, :, lanes(i)] if s == UP else v_hbm.at[rows - 2:rows, :, lanes(i)]
+        src = v_vm.at[0:2, :, lanes(i)] if s == UP else v_vm.at[rows - 2:rows, :, lanes(i)]
         slot = i - CHUNKS + count
         return pltpu.make_async_remote_copy(
             src_ref=src, dst_ref=hop_vm.at[slot], send_sem=row_send.at[s], recv_sem=hop_recv.at[slot],
@@ -84,7 +85,10 @@
         for s in (UP, DOWN):
             detoured = crossing[s] & (i >= CHUNKS - late)
             when(exists(s) & jnp.logical_not(detoured), lambda s=s: row_copy(s, i).start())
-            when(exists(s) & detoured, lambda s=s: hop(s, i, late).start())
+
+    def send_hops(i):
+        for s in (UP, DOWN):
+            when(exists(s) & crossing[s] & (i >= CHUNKS - late), lambda s=s: hop(s, i, late).start())
 
     def hop_on(s, slot):
         i = CHUNKS - held + slot
@@ -93,10 +97,10 @@
             send_sem=hop_send, recv_sem=row_recv.at[i],
             device_id=(gy + (1 if s == UP else -1), gx), device_id_type=MESH)
 
-    def each_held(slots, f):
+    def each_held(slots, f, only=True):
         for s in (UP, DOWN):
             for slot in slots:
-                when(crossing[s] & (slot < held), functools.partial(f, s, slot))
+                when(crossing[s] & (slot < held) & only, functools.partial(f, s, slot))
 
     def hop_pass(s, slot):
         hop(s, CHUNKS - held + slot, held).wait_recv()
@@ -110,36 +114,33 @@
 
     turns = ((gx == TURN + 1), (gx == TURN))
 
-    def detour(s, i):
-        first, second = RELAYS[1 - s]
-        via = jnp.where(i % 3 == 0, first, second)
-        return pltpu.make_async_remote_copy(
-            src_ref=col_out.at[s, :, :, lanes(i)], dst_ref=relay_vm.at[i // 3],
-            send_sem=col_send.at[s], recv_sem=relay_recv.at[i // 3], device_id=(gy, via), device_id_type=MESH)
+    def detour(s, i, n):
+        slot = jnp.where(n == 2, i - 6, i // 3)
+        first, second, third = RELAYS[1 - s]
+        via = jnp.where(n == 2, third, jnp.where(n == 0, first, second))
+        return pltpu.make_async_remote_copy(
+            src_ref=col_out.at[s, :, :, lanes(i)], dst_ref=relay_vm.at[slot],
+            send_sem=col_send.at[s], recv_sem=relay_recv.at[slot], device_id=(gy, via), device_id_type=MESH)
 
     def send_cols(s, i):
-        around = turns[s] & (i % 3 < 2)
+        around = turns[s] & ((i % 3 < 2) | (i >= 6))
         when(exists(LEFT + s) & jnp.logical_not(around), lambda: col_copy(s, i).start())
-        when(around, lambda: detour(s, i).start())
-
-    def forward(s, i):
-        j = 2 - 2 * s
-        return pltpu.make_async_remote_copy(
-            src_ref=relay_vm.at[i // 3], dst_ref=col_vm.at[j:j + 2, 0:rows, lanes(i)],
-            send_sem=relay_send, recv_sem=col_recv.at[s, i // GROUP], device_id=(gy, TURN + s), device_id_type=MESH)
-
-    def relays(f):
+        when(around, lambda: detour(s, i, jnp.where(i >= 6, 2, i % 3)).start())
+
+    def pass_on(slot, late):
         for s in (0, 1):
             for n, via in enumerate(RELAYS[1 - s]):
-                when(gx == via, functools.partial(f, s, n))
-
-    def pass_on(j):
-        def one(s, n):
-            i = n + 3 * j
-            if i < CHUNKS:
-                detour(s, i).wait_recv()
-                forward(s, i).start()
-        relays(one)
+                if late == (n == 2):
+                    i = 6 + slot if late else n + 3 * slot
+
+                    def one(s=s, n=n, i=i):
+                        detour(s, i, n).wait_recv()
+                        j = 2 - 2 * s
+                        pltpu.make_async_remote_copy(
+                            src_ref=relay_vm.at[slot], dst_ref=col_vm.at[j:j + 2, 0:rows, lanes(i)], send_sem=relay_send,
+                            recv_sem=col_recv.at[s, i // GROUP], device_id=(gy, TURN + s), device_id_type=MESH).start()
+
+                    when(gx == via, one)
 
     def cor_copy(s, i):
         return pltpu.make_async_remote_copy(
@@ -166,8 +167,10 @@
     take_coef = pltpu.make_async_copy(coef_hbm, coef, coef_sem)
     barrier = pltpu.get_barrier_semaphore()
     take_coef.start()
+    load(0, 2, edge_sem.at[0]).start()
+    load(rows - 2, 2, edge_sem.at[1]).start()
     known = jnp.int32(0)
-    for n in range(8):
+    for n in range(4):
         when(exists(n), lambda n=n: pl.semaphore_signal(barrier, inc=1, device_id=at(n), device_id_type=MESH))
         known = known + exists(n).astype(jnp.int32)
     for dy in (-2, 2):
@@ -185,8 +188,7 @@
     col_msg[...] = jnp.zeros_like(col_msg)
     flipped[...] = jnp.zeros_like(flipped)
     take_coef.wait()
-    for q in range(4):
-        load(pl.ds(8 * q, 8)).start()
+    load(2, rows - 4, load_sem).start()
     padded[0:9, :, 0:cols] = coef[...]
     lane = lax.broadcasted_iota(jnp.int32, (8, 128), 1)
     for e, r in ((0, 0), (1, rows - 1)):
@@ -199,16 +201,30 @@
         col_msg[0, g:g + 1, :] = turned[0:1]
         col_msg[1, g:g + 1, :] = turned[cols - 1:cols]
         flipped[g, 1:cols + 1, :] = turned[0:cols]
+    load(0, 2, edge_sem.at[0]).wait()
+    load(rows - 2, 2, edge_sem.at[1]).wait()
     pl.semaphore_wait(barrier, known)
 
-    for n in range(8):
+    for n in (LEFT, RIGHT):
+        when(exists(n), lambda n=n: pl.semaphore_signal(ready_sem, inc=1, device_id=at(n), device_id_type=MESH))
+    for n in range(4):
+        when(exists(n), lambda n=n: msg_copy(n).start())
+    send_rows(0)
+    pl.semaphore_wait(ready_sem, exists(LEFT).astype(jnp.int32) + exists(RIGHT).astype(jnp.int32))
+    for n in range(4, 8):
         when(exists(n), lambda n=n: msg_copy(n).start())
 
     def rest(i, c):
         send_rows(i)
         return c
 
-    lax.fori_loop(0, CHUNKS, rest, 0)
+    def hops(i, c):
+        send_hops(i)
+        return c
+
+    lax.fori_loop(2, CHUNKS, hops, 0)
+
+    lax.fori_loop(1, CHUNKS - 3, rest, 0)
 
     def clear(ref):
         ref[...] = jnp.zeros_like(ref)
@@ -229,7 +245,7 @@
             send_cols(s, i)
         return c
 
-    load(pl.ds(0, rows)).wait()
+    load(2, rows - 4, load_sem).wait()
     lax.fori_loop(0, CHUNKS, pack, 0)
     for n in range(4, 8):
         dy, dx = STEPS[n]
@@ -355,12 +371,17 @@
                 t_lo[b, rl * 32:rl * 32 + 32, tile * 128:tile * 128 + 128] = (x - hi.astype(F32)).astype(BF16)
         return c
 
+    each_held((0, 1), hop_pass, held > 2)
+    send_rows(CHUNKS - 3)
     lax.fori_loop(0, 2, build, 0)
-    pass_on(0)
-    each_held((0, 1), hop_pass)
+    pass_on(0, False)
+    each_held((2,), hop_pass)
+    send_rows(CHUNKS - 2)
     lax.fori_loop(2, 4, build, 0)
-    pass_on(1)
-    each_held((2,), hop_pass)
+    pass_on(1, False)
+    each_held((3,), hop_pass)
+    each_held((0, 1), hop_pass, held == 2)
+    send_rows(CHUNKS - 1)
 
     def halves(x):
         hi = x.astype(BF16)
@@ -415,12 +436,19 @@
             y = products(t_hi[q], t_lo[q], w_hi[i % SETS, q], w_lo[i % SETS, q])
             image_ref[8 * q:8 * q + 8, :, lanes(i)] = y.reshape(8, cols, width)
 
+    turned = turns[0] | turns[1]
+
+    def computed(i):
+        late_count = jnp.clip(i - 2, 0, CHUNKS - LAG)
+        return jnp.where(turned | (i < CHUNKS - 3), late_count, jnp.minimum(i - 1, CHUNKS - LAG))
+
     def main(i, c):
-        for step, slots in ((1, (3,)), (2, (4,)), (3, (5,))):
+        for step, slots in ((1, (4,)), (2, (5,))):
             when(i == step, lambda slots=slots: each_held(slots, hop_pass))
-        when(i == 2, lambda: pass_on(2))
+        for step in (3, 4):
+            when(i == step, functools.partial(pass_on, step - 3, True))
         own_part(i)
-        when(i >= LAG, lambda: compute(i - LAG))
+        lax.fori_loop(computed(i - 1), computed(i), lambda c, x: (compute(c), x)[1], 0)
         both_or_one(UP, DOWN, row_vm.at[:, :, :, lanes(i)], up_vm.at[:, :, lanes(i)], row_recv, i)
         for s in (0, 1):
             for j in (0, 1):
@@ -459,25 +487,24 @@
     return y + jnp.dot(t_hi, w_lo, preferred_element_type=F32)
 
 
-def last_chunks(normal_vm, image_vm, t_hi, t_lo, w_hi, w_lo, normal_hbm, image_hbm, tail, normal_sem, image_sem, tail_sem):
+def last_chunks(normal_vm, image_vm, t_hi, t_lo, w_hi, w_lo, normal_hbm, image_hbm, tail, normal_sem, image_sem):
     rows, cols, nv = image_hbm.shape
     width = nv // CHUNKS
     done = nv - LAG * width
-    copies = [pltpu.make_async_copy(
-        image_vm.at[8 * q:8 * q + 8, :, :], image_hbm.at[8 * q:8 * q + 8, :, 0:done], image_sem.at[q]) for q in range(4)]
-    copies.append(pltpu.make_async_copy(normal_vm, normal_hbm, normal_sem))
-    for copy in copies:
-        copy.start()
+    for q in range(4):
+        pltpu.make_async_copy(
+            image_vm.at[8 * q:8 * q + 8, :, :], image_hbm.at[8 * q:8 * q + 8, :, 0:done], image_sem).start()
+    write_normal = pltpu.make_async_copy(normal_vm, normal_hbm, normal_sem)
+    write_normal.start()
     for n in range(LAG):
         i = CHUNKS - LAG + n
         for q in range(4):
             y = products(t_hi[q], t_lo[q], w_hi[i % SETS, q], w_lo[i % SETS, q])
             tail[n, q] = y.reshape(8, cols, width)
-            copies.append(pltpu.make_async_copy(
-                tail.at[n, q], image_hbm.at[8 * q:8 * q + 8, :, i * width:i * width + width], tail_sem.at[n, q]))
-            copies[-1].start()
-    for copy in copies:
-        copy.wait()
+            pltpu.make_async_copy(
+                tail.at[n, q], image_hbm.at[8 * q:8 * q + 8, :, i * width:i * width + width], image_sem).start()
+    pltpu.make_async_copy(image_hbm, image_hbm, image_sem).wait()
+    write_normal.wait()
 
 
 def per_device(rows_total, cols_total, coefficients, vectors):
@@ -505,19 +532,19 @@
             pltpu.VMEM((2, 2, rows, nv), F32),
             pltpu.VMEM((2, 8, nv), F32),
             pltpu.VMEM((2, 8, nv), F32),
-            pltpu.VMEM((3, 2, rows, width), F32),
+            pltpu.VMEM((2, 2, rows, width), F32),
             pltpu.VMEM((6, 2, cols, width), F32),
             pltpu.VMEM((4, 4, NEAR * width), F32),
             pltpu.VMEM((4, 4, NEAR * width), F32),
             pltpu.VMEM((2, 8, 128), F32),
             pltpu.VMEM((2, 8, 128), F32),
             pltpu.VMEM((8, 8, 128), F32),
-            dma, dma,
+            dma, dma((2,)), pltpu.SemaphoreType.REGULAR, dma,
             dma, dma,
             dma((2,)), dma((CHUNKS,)),
             dma((2,)), dma((2, CHUNKS // GROUP)),
             dma((2,)), dma((CHUNKS - NEAR,)),
-            dma((3,)), dma,
+            dma((2,)), dma,
             dma((6,)), dma,
             dma, dma,
         ],
@@ -528,7 +555,7 @@
         out_shape=(jax.ShapeDtypeStruct((25, rows, cols), F32), jax.ShapeDtypeStruct((rows, cols, nv), F32)),
         in_specs=[pl.BlockSpec(memory_space=pltpu.VMEM)] * 6,
         out_specs=(pl.BlockSpec(memory_space=pltpu.HBM),) * 2,
-        scratch_shapes=[pltpu.VMEM((LAG, 4, 8, cols, width), F32), dma, dma((4,)), dma((LAG, 4))],
+        scratch_shapes=[pltpu.VMEM((LAG, 4, 8, cols, width), F32), dma, dma],
         compiler_params=pltpu.CompilerParams(vmem_limit_bytes=8 * 2**20),
     )(*parts)
 

time: 34.8 us -> 34.2 us (0.983)
  the two profiles are of different devices: /device:TPU:43 before, /device:TPU:39 now
where the time goes in v6:
time: 34.2 us; the launch traced here: 33.8 us
  Pallas kernels  33.2 us (97%)
  between operations  0.64 us (2%)
    pallas_call x1, Pallas kernels, per_device(): pl.pallas_call(functools.partial(kernel, rows_total, cols_total), out_sha...  29.7 us
    pallas_call x1, Pallas kernels, per_device(): pl.pallas_call(last_chunks, out_shape=(jax.ShapeDtypeStruct((25, rows, co...  3.43 us

profile of v6, /device:TPU:39, one launch (start us, length us, event | category | flops | bytes accessed | tf_op | source)
XLA Modules:
  0.0 33.8 jit_solution(9006311620454448328)
XLA Ops:
  0.6 29.7 %shard_map.41 = (f32[25,32,32]{2,1,0:T(8,128)S(1)}, f32[32,32,1280]{2,1,0:T(8,128)S(1)}, bf16[4,256,512]{2,1,0:T(8,128)(2,1)S(1)}, bf16[4,256,512]{2,1,0:T(8,128...) custom-call(f32[9,32,32]{2,1,0:T(8,128)} %coef_hbm.1, f32[32,32,2048]{2,1,0:T(8,128)} %v_hbm.1), custom_call_target="tpu_custom_call" | custom-call | tf_op jit(solution)/shard_map/pallas_call | solution.py:515
  30.4 3.4 %shard_map.42 = (f32[25,32,32]{2,1,0:T(8,128)}, f32[32,32,2048]{2,1,0:T(8,128)}) custom-call(f32[25,32,32]{2,1,0:T(8,128)S(1)} %get-tuple-element.8.normal_vm, f32[32,32,1280]{2,1,0:T(8,128)S(1)} %get-tuple-element.9.image_vm, bf16[4,256,512]{2,1,0:T(8,128)(2,1)S(1)} %get-tuple-element.10.t_hi, bf16[4,256,512]{2,1,0:T(8,128)(2,1)S(1)} %get-tuple-element.11.t_lo, ...), custom_call_target="tpu_custom_call" | custom-call | tf_op jit(solution)/shard_map/pallas_call | solution.py:553

commit v7 on v6

--- a/solution.py
+++ b/solution.py
@@ -16,7 +16,7 @@
 GROUP = 4
 LAG = 3
 SETS = LAG + 1
-NEAR = 2
+NEAR = 3
 SLOTS = [((m // 3 - k // 3) + 2) * 5 + (m % 3 - k % 3) + 2 for k in range(9) for m in range(9)]
 
 

time: 34.2 us -> 33.7 us (0.985)
  Pallas kernels: 33.2 us -> 32.8 us
    pallas_call x1, Pallas kernels: 29.7 us -> 29.4 us  [per_device(): pl.pallas_call(functools.partial(kernel, rows_total, cols_total), out_sha...]
where the time goes in v7:
time: 33.7 us; the launch traced here: 33.4 us
  Pallas kernels  32.8 us (97%)
  between operations  0.64 us (2%)
    pallas_call x1, Pallas kernels, per_device(): pl.pallas_call(functools.partial(kernel, rows_total, cols_total), out_sha...  29.4 us
    pallas_call x1, Pallas kernels, per_device(): pl.pallas_call(last_chunks, out_shape=(jax.ShapeDtypeStruct((25, rows, co...  3.43 us

profile of v7, /device:TPU:39, one launch (start us, length us, event | category | flops | bytes accessed | tf_op | source)
XLA Modules:
  0.0 33.4 jit_solution(9861635132414322454)
XLA Ops:
  0.6 29.4 %shard_map.41 = (f32[25,32,32]{2,1,0:T(8,128)S(1)}, f32[32,32,1280]{2,1,0:T(8,128)S(1)}, bf16[4,256,512]{2,1,0:T(8,128)(2,1)S(1)}, bf16[4,256,512]{2,1,0:T(8,128...) custom-call(f32[9,32,32]{2,1,0:T(8,128)} %coef_hbm.1, f32[32,32,2048]{2,1,0:T(8,128)} %v_hbm.1), custom_call_target="tpu_custom_call" | custom-call | tf_op jit(solution)/shard_map/pallas_call | solution.py:515
  30.0 3.4 %shard_map.42 = (f32[25,32,32]{2,1,0:T(8,128)}, f32[32,32,2048]{2,1,0:T(8,128)}) custom-call(f32[25,32,32]{2,1,0:T(8,128)S(1)} %get-tuple-element.8.normal_vm, f32[32,32,1280]{2,1,0:T(8,128)S(1)} %get-tuple-element.9.image_vm, bf16[4,256,512]{2,1,0:T(8,128)(2,1)S(1)} %get-tuple-element.10.t_hi, bf16[4,256,512]{2,1,0:T(8,128)(2,1)S(1)} %get-tuple-element.11.t_lo, ...), custom_call_target="tpu_custom_call" | custom-call | tf_op jit(solution)/shard_map/pallas_call | solution.py:553
